TPU v7x, 128 devices: a whole 4x4x4 slice. The times are simulated.
128 devices in a mesh: lat: 2 (over x_lo), lon: 8 (over z_lo, x_hi, core), lev: 8 (over z_hi, y).
Axes of the slice: x: 4 (x_hi: 2, x_lo: 2; x = x_hi * 2 + x_lo), y: 4, z: 4 (z_hi: 2, z_lo: 2; z = z_hi * 2 + z_lo), core: 2. Of those that a mesh axis runs over, the one named last changes fastest.
Arguments:
- initial_state: float32 [16, 256, 512, 128], P('lat', 'lon', 'lev'), may hold values from 0.2 to 1.8
- scaled_diffusivity: float32 [16, 256, 512, 128], P('lat', 'lon', 'lev'), may hold values from 0.03 to 0.15
- scaled_forcing: float32 [16, 256, 512, 128], P('lat', 'lon', 'lev'), may hold values from -0.2 to 0.2
Outputs:
- cumulative_totals: float32 [16, 256, 512, 128], P('lat', 'lon', 'lev')
- temperature_end: float32 [16, 256, 512, 128], P('lat', 'lon', 'lev')
All inputs are finite; a program needn't handle non-finite values.
Results may differ from a plain program's by a relative error of at most 0.00002.
Values sent between devices are 32-bit elements; how exact they have to be, the bound alone decides.
A program may use at most 128 MiB of HBM per device.

v0:
```python
import jax
import jax.numpy as jnp
from jax import lax
from jax.sharding import Mesh
from jax.sharding import PartitionSpec as P

STEPS = 4
LON = ("lon_0", "lon_1", "lon_2")


def with_halo(x, sides, width):
    edges = {}
    for axis, dim in sides:
        size, length = (lax.axis_size(axis), x.shape[dim])
        up = [(i, (i + 1) % size) for i in range(size - 1)]
        last = lax.slice_in_dim(x, length - width, length, axis=dim)
        initial = lax.slice_in_dim(x, 0, width, axis=dim)
        edges[dim] = (
            lax.ppermute(last, axis, up),
            lax.ppermute(initial, axis, [(b, a) for a, b in up]),
        )
    done = []
    for _, dim in sides:
        low, high = edges[dim]
        around = [(width, width) if d in done else (0, 0) for d in range(x.ndim)]
        x = jnp.concatenate([jnp.pad(low, around), x, jnp.pad(high, around)], axis=dim)
        done.append(dim)
    return x


def nothing_yet(x, identity):
    return jnp.broadcast_to(jnp.asarray(identity, x.dtype), x.shape)


def prefix_by_axis(x, axes, combine, identity):
    before = start = nothing_yet(x, identity)
    total = x
    for axis in reversed(axes):
        length, here = (lax.axis_size(axis), lax.axis_index(axis))
        pieces = lax.all_gather(total, axis)
        inside, total = (start, start)
        for k in range(length):
            passed = k < here
            total = combine(total, pieces[k])
            inside = jnp.where(passed, total, inside)
        before = combine(inside, before)
    return before


def strip_edges(values, dims):
    for dim in dims:
        values = lax.slice_in_dim(values, 1, values.shape[dim] - 1, axis=dim)
    return values


def neighbour(values, dim, start, dims):
    others = [other for other in dims if other != dim]
    values = strip_edges(values, others)
    return lax.slice_in_dim(values, start, start + values.shape[dim] - 2, axis=dim)


def explicit_update(haloed_values, scaled_diffusivity, scaled_forcing):
    middle = strip_edges(haloed_values, (0, 1, 2))
    lower = [neighbour(haloed_values, dim, 0, (0, 1, 2)) for dim in (0, 1, 2)]
    upper = [neighbour(haloed_values, dim, 2, (0, 1, 2)) for dim in (0, 1, 2)]
    spread = lower[0] + upper[0] + lower[1] + upper[1] + lower[2] + upper[2] - 6.0 * middle
    return middle + scaled_diffusivity * spread + scaled_forcing


def per_device(initial_state, scaled_diffusivity, scaled_forcing):
    for step in range(STEPS):
        haloed_values = with_halo(initial_state, (("lat", 0), (LON, 1), ("lev", 2)), 1)
        initial_state = explicit_update(haloed_values, scaled_diffusivity, scaled_forcing)
    present_layer = jnp.cumsum(initial_state, axis=1)
    total = lax.slice_in_dim(
        present_layer, present_layer.shape[1] - 1, present_layer.shape[1], axis=1
    )

    def add_pair(earlier_total, later_total):
        return earlier_total + later_total

    previous_plane = prefix_by_axis(total, LON, add_pair, jnp.zeros_like(total))
    cumulative_totals = (present_layer + previous_plane) / (
        initial_state.shape[1] * lax.axis_size(LON)
    )
    return (cumulative_totals, initial_state)


def solution(mesh):
    split = Mesh(
        mesh.devices.reshape(mesh.shape["lat"], 2, 2, 2, mesh.shape["lev"]),
        ("lat", "lon_0", "lon_1", "lon_2", "lev"),
    )
    return jax.shard_map(
        per_device,
        mesh=split,
        in_specs=(
            P("lat", LON, "lev", None),
            P("lat", LON, "lev", None),
            P("lat", LON, "lev", None),
        ),
        out_specs=(P("lat", LON, "lev", None), P("lat", LON, "lev", None)),
        check_vma=False,
    )
```

profile of v0, /device:TPU:56, one launch (start us, length us, event | category | flops | bytes accessed | tf_op | source)
XLA Modules:
  0.0 322.7 jit_solution(642423002292479463)
XLA Ops:
  2.5 3.7 %collective-permute-start = (f32[1,32,64,128]{3,2,1,0:T(8,128)S(1)}, f32[1,32,64,128]{3,2,1,0:T(8,128)S(1)}, u32[]{:S(2)}, u32[]{:S(2)}) collective-permute-start(f32[1,32,64,128]{3,2,1,0:T(8,128)S(1)} %get-tuple-element.27), channel_id=1, source_target_pairs={{0,64},{1,65},{2,66},{3,67},{4,68},{5,69},{6,70},{7,71},{8,72},{9,... | collective-permute-start | bytes 3145736 | tf_op jit(solution)/shard_map/ppermute | solution.py:19
  10.5 6.0 %collective-permute-start.3 = (f32[8,1,64,128]{3,2,1,0:T(8,128)S(1)}, f32[8,1,64,128]{3,2,1,0:T(8,128)S(1)}, u32[]{:S(2)}, u32[]{:S(2)}) collective-permute-start(f32[8,1,64,128]{3,2,1,0:T(8,128)S(1)} %get-tuple-element.25), channel_id=1, source_target_pairs={{8,0},{16,8},{24,16},{32,24},{40,32},{48,40},{56,48},{9,1},{17,9},... | collective-permute-start | bytes 786440 | tf_op jit(solution)/shard_map/ppermute | solution.py:20
  16.6 2.5 fusion.57
  19.0 4.5 %collective-permute-start.4 = (f32[8,32,1,128]{3,1,2,0:T(8,128)}, f32[8,32,1,128]{3,1,2,0:T(8,128)S(1)}, u32[]{:S(2)}, u32[]{:S(2)}) collective-permute-start(f32[8,32,1,128]{3,1,2,0:T(8,128)} %bitcast.22), channel_id=1, source_target_pairs={{0,1},{1,2},{2,3},{3,4},{4,5},{5,6},{6,7},{8,9},{9,10},{10,11},{11... | collective-permute-start | bytes 393224 | tf_op jit(solution)/shard_map/ppermute | solution.py:19
  23.6 12.2 %collective-permute-done.2 = f32[8,1,64,128]{3,2,1,0:T(8,128)S(1)} collective-permute-done((f32[8,1,64,128]{3,2,1,0:T(8,128)S(1)}, f32[8,1,64,128]{3,2,1,0:T(8,128)S(1)}, u32[]{:S(2)}, u32[]{:S(2)}) %collective-permute-start.2) | collective-permute-done | bytes 262176 | tf_op jit(solution)/shard_map/ppermute | solution.py:19
  35.8 2.6 collective-permute-start.5
  40.3 4.7 %constant_dynamic-update-slice_fusion.1 = f32[10,32,64,128]{3,2,1,0:T(8,128)} fusion(f32[10,32,64,128]{3,2,1,0:T(8,128)} %constant_dynamic-update-slice_fusion.2, f32[8,32,64,128]{3,2,1,0:T(8,128)S(1)} %copy-done), kind=kLoop, calls=%fused_computation.123 | loop fusion | bytes 16777216
  47.1 30.1 %fusion.38 = f32[8,32,64,128]{3,2,1,0:T(8,128)} fusion(f32[8,32,64,128]{3,2,1,0:T(8,128)S(1)} %bitcast.43, f32[8,32,64,128]{3,2,1,0:T(8,128)} %param.3, f32[8,32,64,128]{3,2,1,0:T(8,128)} %param.4, f32[8,32,1,128]{3,2,1,0:T(1,128)} %bitcast.25, f32[10,1,64,128]{3,2,1,0:T(8,128)} %pad.51, f32[10,32,64,128]{3,2,1,0:T(8,128)} %constant_dynamic-update-slice_fusion, ...), kind=kLoop, calls=%fused_computation.93 | loop fusion | flops 54525952 | bytes 47054848 | tf_op jit(solution)/shard_map/add | solution.py:67
  78.8 4.8 %collective-permute-start.6 = (f32[1,32,64,128]{3,2,1,0:T(8,128)S(1)}, f32[1,32,64,128]{3,2,1,0:T(8,128)S(1)}, u32[]{:S(2)}, u32[]{:S(2)}) collective-permute-start(f32[1,32,64,128]{3,2,1,0:T(8,128)S(1)} %get-tuple-element.18), channel_id=1, source_target_pairs={{0,64},{1,65},{2,66},{3,67},{4,68},{5,69},{6,70},{7,71},{8,72},{9,... | collective-permute-start | bytes 3145736 | tf_op jit(solution)/shard_map/ppermute | solution.py:19
  88.0 6.0 %collective-permute-start.9 = (f32[8,1,64,128]{3,2,1,0:T(8,128)S(1)}, f32[8,1,64,128]{3,2,1,0:T(8,128)S(1)}, u32[]{:S(2)}, u32[]{:S(2)}) collective-permute-start(f32[8,1,64,128]{3,2,1,0:T(8,128)S(1)} %get-tuple-element.21), channel_id=1, source_target_pairs={{8,0},{16,8},{24,16},{32,24},{40,32},{48,40},{56,48},{9,1},{17,9},... | collective-permute-start | bytes 786440 | tf_op jit(solution)/shard_map/ppermute | solution.py:20
  95.8 6.8 %collective-permute-start.10 = (f32[8,32,1,128]{3,1,2,0:T(8,128)S(1)}, f32[8,32,1,128]{3,1,2,0:T(8,128)S(1)}, u32[]{:S(2)}, u32[]{:S(2)}) collective-permute-start(f32[8,32,1,128]{3,1,2,0:T(8,128)S(1)} %bitcast.55), channel_id=1, source_target_pairs={{0,1},{1,2},{2,3},{3,4},{4,5},{5,6},{6,7},{8,9},{9,10},{10,11},{11... | collective-permute-start | bytes 393224 | tf_op jit(solution)/shard_map/ppermute | solution.py:19
  102.6 11.2 %collective-permute-done.8 = f32[8,1,64,128]{3,2,1,0:T(8,128)S(1)} collective-permute-done((f32[8,1,64,128]{3,2,1,0:T(8,128)S(1)}, f32[8,1,64,128]{3,2,1,0:T(8,128)S(1)}, u32[]{:S(2)}, u32[]{:S(2)}) %collective-permute-start.8) | collective-permute-done | bytes 262176 | tf_op jit(solution)/shard_map/ppermute | solution.py:19
  113.8 2.3 collective-permute-start.11
  116.2 8.0 %collective-permute-done.11 = f32[8,32,1,128]{3,1,2,0:T(8,128)S(1)} collective-permute-done((f32[8,32,1,128]{3,1,2,0:T(8,128)S(1)}, f32[8,32,1,128]{3,1,2,0:T(8,128)S(1)}, u32[]{:S(2)}, u32[]{:S(2)}) %collective-permute-start.11) | collective-permute-done | bytes 131104 | tf_op jit(solution)/shard_map/ppermute | solution.py:20
  124.3 28.3 %fusion.27 = f32[8,32,64,128]{3,2,1,0:T(8,128)} fusion(f32[8,32,64,128]{3,2,1,0:T(8,128)} %param.5, f32[8,32,64,128]{3,2,1,0:T(8,128)} %fusion.38, f32[8,32,64,128]{3,2,1,0:T(8,128)} %param.4, f32[8,32,1,128]{3,2,1,0:T(1,128)S(1)} %bitcast.51, f32[10,1,64,128]{3,2,1,0:T(8,128)S(1)} %pad.55, f32[10,1,64,128]{3,2,1,0:T(8,128)S(1)} %pad.54, ...), kind=kLoop, calls=%fused_computation.64 | loop fusion | flops 71303168 | bytes 36569088 | tf_op jit(solution)/shard_map/add | solution.py:67
  154.3 5.4 %collective-permute-start.12 = (f32[1,32,64,128]{3,2,1,0:T(8,128)S(1)}, f32[1,32,64,128]{3,2,1,0:T(8,128)S(1)}, u32[]{:S(2)}, u32[]{:S(2)}) collective-permute-start(f32[1,32,64,128]{3,2,1,0:T(8,128)S(1)} %get-tuple-element.12), channel_id=1, source_target_pairs={{0,64},{1,65},{2,66},{3,67},{4,68},{5,69},{6,70},{7,71},{8,72},{9,... | collective-permute-start | bytes 3145736 | tf_op jit(solution)/shard_map/ppermute | solution.py:19
  164.0 6.0 %collective-permute-start.15 = (f32[8,1,64,128]{3,2,1,0:T(8,128)S(1)}, f32[8,1,64,128]{3,2,1,0:T(8,128)S(1)}, u32[]{:S(2)}, u32[]{:S(2)}) collective-permute-start(f32[8,1,64,128]{3,2,1,0:T(8,128)S(1)} %get-tuple-element.15), channel_id=1, source_target_pairs={{8,0},{16,8},{24,16},{32,24},{40,32},{48,40},{56,48},{9,1},{17,9},... | collective-permute-start | bytes 786440 | tf_op jit(solution)/shard_map/ppermute | solution.py:20
  173.7 6.4 %collective-permute-done.14 = f32[8,1,64,128]{3,2,1,0:T(8,128)S(1)} collective-permute-done((f32[8,1,64,128]{3,2,1,0:T(8,128)S(1)}, f32[8,1,64,128]{3,2,1,0:T(8,128)S(1)}, u32[]{:S(2)}, u32[]{:S(2)}) %collective-permute-start.14) | collective-permute-done | bytes 262176 | tf_op jit(solution)/shard_map/ppermute | solution.py:19
  182.4 8.3 %collective-permute-done.17 = f32[8,32,1,128]{3,1,2,0:T(8,128)S(1)} collective-permute-done((f32[8,32,1,128]{3,1,2,0:T(8,128)S(1)}, f32[8,32,1,128]{3,1,2,0:T(8,128)S(1)}, u32[]{:S(2)}, u32[]{:S(2)}) %collective-permute-start.17) | collective-permute-done | bytes 131104 | tf_op jit(solution)/shard_map/ppermute | solution.py:20
  190.6 28.4 %fusion.16 = f32[8,32,64,128]{3,2,1,0:T(8,128)} fusion(f32[8,32,64,128]{3,2,1,0:T(8,128)} %param.5, f32[8,32,64,128]{3,2,1,0:T(8,128)} %fusion.27, f32[8,32,64,128]{3,2,1,0:T(8,128)} %param.4, f32[8,32,1,128]{3,2,1,0:T(1,128)S(1)} %bitcast.52, f32[10,1,64,128]{3,2,1,0:T(8,128)S(1)} %pad.59, f32[10,1,64,128]{3,2,1,0:T(8,128)S(1)} %pad.58, ...), kind=kLoop, calls=%fused_computation.35 | loop fusion | flops 71303168 | bytes 36569088 | tf_op jit(solution)/shard_map/add | solution.py:67
  219.0 2.7 fusion.49
  221.7 5.4 %collective-permute-start.18 = (f32[1,32,64,128]{3,2,1,0:T(8,128)}, f32[1,32,64,128]{3,2,1,0:T(8,128)S(1)}, u32[]{:S(2)}, u32[]{:S(2)}) collective-permute-start(f32[1,32,64,128]{3,2,1,0:T(8,128)} %get-tuple-element.6), channel_id=1, source_target_pairs={{0,64},{1,65},{2,66},{3,67},{4,68},{5,69},{6,70},{7,71},{8,72},{9,... | collective-permute-start | bytes 3145736 | tf_op jit(solution)/shard_map/ppermute | solution.py:19
  232.1 6.0 %collective-permute-start.21 = (f32[8,1,64,128]{3,2,1,0:T(8,128)}, f32[8,1,64,128]{3,2,1,0:T(8,128)S(1)}, u32[]{:S(2)}, u32[]{:S(2)}) collective-permute-start(f32[8,1,64,128]{3,2,1,0:T(8,128)} %get-tuple-element.9), channel_id=1, source_target_pairs={{8,0},{16,8},{24,16},{32,24},{40,32},{48,40},{56,48},{9,1},{17,9},... | collective-permute-start | bytes 786440 | tf_op jit(solution)/shard_map/ppermute | solution.py:20
  238.1 2.5 fusion.48
  242.5 5.4 %collective-permute-done.20 = f32[8,1,64,128]{3,2,1,0:T(8,128)} collective-permute-done((f32[8,1,64,128]{3,2,1,0:T(8,128)S(1)}, f32[8,1,64,128]{3,2,1,0:T(8,128)}, u32[]{:S(2)}, u32[]{:S(2)}) %collective-permute-start.20) | collective-permute-done | bytes 262176 | tf_op jit(solution)/shard_map/ppermute | solution.py:19
  251.3 3.8 %collective-permute-done.22 = f32[8,32,1,128]{3,1,2,0:T(8,128)} collective-permute-done((f32[8,32,1,128]{3,1,2,0:T(8,128)}, f32[8,32,1,128]{3,1,2,0:T(8,128)}, u32[]{:S(2)}, u32[]{:S(2)}) %collective-permute-start.22) | collective-permute-done | bytes 131104 | tf_op jit(solution)/shard_map/ppermute | solution.py:19
  255.1 28.4 %fusion.5 = f32[8,32,64,128]{3,2,1,0:T(8,128)} fusion(f32[8,32,64,128]{3,2,1,0:T(8,128)} %param.5, f32[8,32,64,128]{3,2,1,0:T(8,128)} %fusion.16, f32[8,32,64,128]{3,2,1,0:T(8,128)} %param.4, f32[8,32,1,128]{3,2,1,0:T(1,128)S(1)} %bitcast.47, f32[10,1,64,128]{3,2,1,0:T(8,128)S(1)} %pad.63, f32[10,1,64,128]{3,2,1,0:T(8,128)S(1)} %pad.62, ...), kind=kLoop, calls=%fused_computation.6 | loop fusion | flops 71303168 | bytes 36569088 | tf_op jit(solution)/shard_map/add | solution.py:67
  283.4 8.4 %fusion.60 = f32[8,32,64,128]{3,2,1,0:T(8,128)} fusion(f32[8,32,64,128]{3,2,1,0:T(8,128)} %fusion.5), kind=kOutput, calls=%fused_computation.137 | output fusion | flops 65011712 | bytes 16777216 | tf_op jit(solution)/shard_map/jit(cumsum)/reduce_window_sum | solution.py:74
  292.8 2.2 all-gather
  295.1 10.5 %all-gather.1 = f32[16,1,64,128]{3,2,1,0:T(8,128)S(1)} all-gather(f32[8,1,64,128]{3,2,1,0:T(8,128)S(1)} %slice_add_fusion.2), channel_id=3, replica_groups=mesh['lat'=2,'lon_0'=2,'lon_1'=2,'lon_2'=2,'lev'=8] {'lon_1'}, dimensions={0}, use_global_device_ids=true | all-gather | bytes 786432 | tf_op jit(solution)/shard_map/all_gather | solution.py:40
  305.6 8.2 %all_gather.17 = f32[2,8,1,64,128]{4,3,2,1,0:T(8,128)S(1)} all-gather(f32[1,8,1,64,128]{4,3,2,1,0:T(8,128)S(1)} %fusion.47), channel_id=1, replica_groups=mesh['lat'=2,'lon_0'=2,'lon_1'=2,'lon_2'=2,'lev'=8] {'lon_0'}, dimensions={0}, use_global_device_ids=true | all-gather | bytes 786432 | tf_op jit(solution)/shard_map/all_gather | solution.py:40
  313.9 8.8 %add_multiply_fusion = f32[8,32,64,128]{3,2,1,0:T(8,128)} fusion(f32[8,32,64,128]{3,2,1,0:T(8,128)} %fusion.60, f32[8,64,128]{2,1,0:T(8,128)S(1)} %fusion.46), kind=kLoop, calls=%fused_computation.110 | loop fusion | flops 4194304 | bytes 17039360 | tf_op jit(solution)/shard_map/div | solution.py:83
  (61 shorter events, 41.0 us)
Async XLA Ops:
  0.6 39.7 %copy-start = (f32[8,32,64,128]{3,2,1,0:T(8,128)S(1)}, f32[8,32,64,128]{3,2,1,0:T(8,128)}, u32[]{:S(2)}) copy-start(f32[8,32,64,128]{3,2,1,0:T(8,128)} %param.3) | copy-start | bytes 25165828
  2.5 36.7 %collective-permute-start = (f32[1,32,64,128]{3,2,1,0:T(8,128)S(1)}, f32[1,32,64,128]{3,2,1,0:T(8,128)S(1)}, u32[]{:S(2)}, u32[]{:S(2)}) collective-permute-start(f32[1,32,64,128]{3,2,1,0:T(8,128)S(1)} %get-tuple-element.27), channel_id=1, source_target_pairs={{0,64},{1,65},{2,66},{3,67},{4,68},{5,69},{6,70},{7,71},{8,72},{9,... | collective-permute-start | bytes 3145736 | tf_op jit(solution)/shard_map/ppermute | solution.py:19
  6.2 38.8 %collective-permute-start.1 = (f32[1,32,64,128]{3,2,1,0:T(8,128)S(1)}, f32[1,32,64,128]{3,2,1,0:T(8,128)S(1)}, u32[]{:S(2)}, u32[]{:S(2)}) collective-permute-start(f32[1,32,64,128]{3,2,1,0:T(8,128)S(1)} %get-tuple-element.26), channel_id=1, source_target_pairs={{64,0},{65,1},{66,2},{67,3},{68,4},{69,5},{70,6},{71,7},{72,8},{73... | collective-permute-start | bytes 3145736 | tf_op jit(solution)/shard_map/ppermute | solution.py:20
  8.6 27.2 %collective-permute-start.2 = (f32[8,1,64,128]{3,2,1,0:T(8,128)S(1)}, f32[8,1,64,128]{3,2,1,0:T(8,128)S(1)}, u32[]{:S(2)}, u32[]{:S(2)}) collective-permute-start(f32[8,1,64,128]{3,2,1,0:T(8,128)S(1)} %get-tuple-element.24), channel_id=1, source_target_pairs={{0,8},{8,16},{16,24},{24,32},{32,40},{40,48},{48,56},{1,9},{9,17},... | collective-permute-start | bytes 786440 | tf_op jit(solution)/shard_map/ppermute | solution.py:19
  10.5 27.9 %collective-permute-start.3 = (f32[8,1,64,128]{3,2,1,0:T(8,128)S(1)}, f32[8,1,64,128]{3,2,1,0:T(8,128)S(1)}, u32[]{:S(2)}, u32[]{:S(2)}) collective-permute-start(f32[8,1,64,128]{3,2,1,0:T(8,128)S(1)} %get-tuple-element.25), channel_id=1, source_target_pairs={{8,0},{16,8},{24,16},{32,24},{40,32},{48,40},{56,48},{9,1},{17,9},... | collective-permute-start | bytes 786440 | tf_op jit(solution)/shard_map/ppermute | solution.py:20
  19.0 28.0 %collective-permute-start.4 = (f32[8,32,1,128]{3,1,2,0:T(8,128)}, f32[8,32,1,128]{3,1,2,0:T(8,128)S(1)}, u32[]{:S(2)}, u32[]{:S(2)}) collective-permute-start(f32[8,32,1,128]{3,1,2,0:T(8,128)} %bitcast.22), channel_id=1, source_target_pairs={{0,1},{1,2},{2,3},{3,4},{4,5},{5,6},{6,7},{8,9},{9,10},{10,11},{11... | collective-permute-start | bytes 393224 | tf_op jit(solution)/shard_map/ppermute | solution.py:19
  35.8 11.3 %collective-permute-start.5 = (f32[8,32,1,128]{3,1,2,0:T(8,128)}, f32[8,32,1,128]{3,1,2,0:T(8,128)}, u32[]{:S(2)}, u32[]{:S(2)}) collective-permute-start(f32[8,32,1,128]{3,1,2,0:T(8,128)} %bitcast.24), channel_id=1, source_target_pairs={{1,0},{2,1},{3,2},{4,3},{5,4},{6,5},{7,6},{9,8},{10,9},{11,10},{12... | collective-permute-start | bytes 393224 | tf_op jit(solution)/shard_map/ppermute | solution.py:20
  39.2 7.8 %slice-start = ((s8[8388608]{0:T(1024)(128)(4,1)}), s8[4194304]{0:T(1024)(128)(4,1)S(1)}, s32[]{:S(2)}) async-start(s8[8388608]{0:T(1024)(128)(4,1)} %bitcast.42), calls=%async_computation | async-start | bytes 8388608
  40.3 6.7 %slice-start.1 = ((s8[8388608]{0:T(1024)(128)(4,1)}), s8[4194304]{0:T(1024)(128)(4,1)S(1)}, s32[]{:S(2)}) async-start(s8[8388608]{0:T(1024)(128)(4,1)} %bitcast.42), calls=%async_computation.1 | async-start | bytes 8388608
  45.0 1.0 copy-start.1
  78.8 45.4 %collective-permute-start.6 = (f32[1,32,64,128]{3,2,1,0:T(8,128)S(1)}, f32[1,32,64,128]{3,2,1,0:T(8,128)S(1)}, u32[]{:S(2)}, u32[]{:S(2)}) collective-permute-start(f32[1,32,64,128]{3,2,1,0:T(8,128)S(1)} %get-tuple-element.18), channel_id=1, source_target_pairs={{0,64},{1,65},{2,66},{3,67},{4,68},{5,69},{6,70},{7,71},{8,72},{9,... | collective-permute-start | bytes 3145736 | tf_op jit(solution)/shard_map/ppermute | solution.py:19
  83.6 40.6 %collective-permute-start.7 = (f32[1,32,64,128]{3,2,1,0:T(8,128)S(1)}, f32[1,32,64,128]{3,2,1,0:T(8,128)S(1)}, u32[]{:S(2)}, u32[]{:S(2)}) collective-permute-start(f32[1,32,64,128]{3,2,1,0:T(8,128)S(1)} %get-tuple-element.19), channel_id=1, source_target_pairs={{64,0},{65,1},{66,2},{67,3},{68,4},{69,5},{70,6},{71,7},{72,8},{73... | collective-permute-start | bytes 3145736 | tf_op jit(solution)/shard_map/ppermute | solution.py:20
  86.0 27.8 %collective-permute-start.8 = (f32[8,1,64,128]{3,2,1,0:T(8,128)S(1)}, f32[8,1,64,128]{3,2,1,0:T(8,128)S(1)}, u32[]{:S(2)}, u32[]{:S(2)}) collective-permute-start(f32[8,1,64,128]{3,2,1,0:T(8,128)S(1)} %get-tuple-element.20), channel_id=1, source_target_pairs={{0,8},{8,16},{16,24},{24,32},{32,40},{40,48},{48,56},{1,9},{9,17},... | collective-permute-start | bytes 786440 | tf_op jit(solution)/shard_map/ppermute | solution.py:19
  88.0 28.2 %collective-permute-start.9 = (f32[8,1,64,128]{3,2,1,0:T(8,128)S(1)}, f32[8,1,64,128]{3,2,1,0:T(8,128)S(1)}, u32[]{:S(2)}, u32[]{:S(2)}) collective-permute-start(f32[8,1,64,128]{3,2,1,0:T(8,128)S(1)} %get-tuple-element.21), channel_id=1, source_target_pairs={{8,0},{16,8},{24,16},{32,24},{40,32},{48,40},{56,48},{9,1},{17,9},... | collective-permute-start | bytes 786440 | tf_op jit(solution)/shard_map/ppermute | solution.py:20
  95.8 20.5 %collective-permute-start.10 = (f32[8,32,1,128]{3,1,2,0:T(8,128)S(1)}, f32[8,32,1,128]{3,1,2,0:T(8,128)S(1)}, u32[]{:S(2)}, u32[]{:S(2)}) collective-permute-start(f32[8,32,1,128]{3,1,2,0:T(8,128)S(1)} %bitcast.55), channel_id=1, source_target_pairs={{0,1},{1,2},{2,3},{3,4},{4,5},{5,6},{6,7},{8,9},{9,10},{10,11},{11... | collective-permute-start | bytes 393224 | tf_op jit(solution)/shard_map/ppermute | solution.py:19
  113.8 10.5 %collective-permute-start.11 = (f32[8,32,1,128]{3,1,2,0:T(8,128)S(1)}, f32[8,32,1,128]{3,1,2,0:T(8,128)S(1)}, u32[]{:S(2)}, u32[]{:S(2)}) collective-permute-start(f32[8,32,1,128]{3,1,2,0:T(8,128)S(1)} %bitcast.53), channel_id=1, source_target_pairs={{1,0},{2,1},{3,2},{4,3},{5,4},{6,5},{7,6},{9,8},{10,9},{11,10},{12... | collective-permute-start | bytes 393224 | tf_op jit(solution)/shard_map/ppermute | solution.py:20
  154.3 36.3 %collective-permute-start.12 = (f32[1,32,64,128]{3,2,1,0:T(8,128)S(1)}, f32[1,32,64,128]{3,2,1,0:T(8,128)S(1)}, u32[]{:S(2)}, u32[]{:S(2)}) collective-permute-start(f32[1,32,64,128]{3,2,1,0:T(8,128)S(1)} %get-tuple-element.12), channel_id=1, source_target_pairs={{0,64},{1,65},{2,66},{3,67},{4,68},{5,69},{6,70},{7,71},{8,72},{9,... | collective-permute-start | bytes 3145736 | tf_op jit(solution)/shard_map/ppermute | solution.py:19
  159.7 31.0 %collective-permute-start.13 = (f32[1,32,64,128]{3,2,1,0:T(8,128)S(1)}, f32[1,32,64,128]{3,2,1,0:T(8,128)S(1)}, u32[]{:S(2)}, u32[]{:S(2)}) collective-permute-start(f32[1,32,64,128]{3,2,1,0:T(8,128)S(1)} %get-tuple-element.13), channel_id=1, source_target_pairs={{64,0},{65,1},{66,2},{67,3},{68,4},{69,5},{70,6},{71,7},{72,8},{73... | collective-permute-start | bytes 3145736 | tf_op jit(solution)/shard_map/ppermute | solution.py:20
  162.1 18.1 %collective-permute-start.14 = (f32[8,1,64,128]{3,2,1,0:T(8,128)S(1)}, f32[8,1,64,128]{3,2,1,0:T(8,128)S(1)}, u32[]{:S(2)}, u32[]{:S(2)}) collective-permute-start(f32[8,1,64,128]{3,2,1,0:T(8,128)S(1)} %get-tuple-element.14), channel_id=1, source_target_pairs={{0,8},{8,16},{16,24},{24,32},{32,40},{40,48},{48,56},{1,9},{9,17},... | collective-permute-start | bytes 786440 | tf_op jit(solution)/shard_map/ppermute | solution.py:19
  164.0 18.3 %collective-permute-start.15 = (f32[8,1,64,128]{3,2,1,0:T(8,128)S(1)}, f32[8,1,64,128]{3,2,1,0:T(8,128)S(1)}, u32[]{:S(2)}, u32[]{:S(2)}) collective-permute-start(f32[8,1,64,128]{3,2,1,0:T(8,128)S(1)} %get-tuple-element.15), channel_id=1, source_target_pairs={{8,0},{16,8},{24,16},{32,24},{40,32},{48,40},{56,48},{9,1},{17,9},... | collective-permute-start | bytes 786440 | tf_op jit(solution)/shard_map/ppermute | solution.py:20
  171.8 10.5 %collective-permute-start.16 = (f32[8,32,1,128]{3,1,2,0:T(8,128)S(1)}, f32[8,32,1,128]{3,1,2,0:T(8,128)S(1)}, u32[]{:S(2)}, u32[]{:S(2)}) collective-permute-start(f32[8,32,1,128]{3,1,2,0:T(8,128)S(1)} %bitcast.56), channel_id=1, source_target_pairs={{0,1},{1,2},{2,3},{3,4},{4,5},{5,6},{6,7},{8,9},{9,10},{10,11},{11... | collective-permute-start | bytes 393224 | tf_op jit(solution)/shard_map/ppermute | solution.py:19
  180.2 10.5 %collective-permute-start.17 = (f32[8,32,1,128]{3,1,2,0:T(8,128)S(1)}, f32[8,32,1,128]{3,1,2,0:T(8,128)S(1)}, u32[]{:S(2)}, u32[]{:S(2)}) collective-permute-start(f32[8,32,1,128]{3,1,2,0:T(8,128)S(1)} %bitcast.54), channel_id=1, source_target_pairs={{1,0},{2,1},{3,2},{4,3},{5,4},{6,5},{7,6},{9,8},{10,9},{11,10},{12... | collective-permute-start | bytes 393224 | tf_op jit(solution)/shard_map/ppermute | solution.py:20
  221.7 33.3 %collective-permute-start.18 = (f32[1,32,64,128]{3,2,1,0:T(8,128)}, f32[1,32,64,128]{3,2,1,0:T(8,128)S(1)}, u32[]{:S(2)}, u32[]{:S(2)}) collective-permute-start(f32[1,32,64,128]{3,2,1,0:T(8,128)} %get-tuple-element.6), channel_id=1, source_target_pairs={{0,64},{1,65},{2,66},{3,67},{4,68},{5,69},{6,70},{7,71},{8,72},{9,... | collective-permute-start | bytes 3145736 | tf_op jit(solution)/shard_map/ppermute | solution.py:19
  227.1 28.0 %collective-permute-start.19 = (f32[1,32,64,128]{3,2,1,0:T(8,128)S(1)}, f32[1,32,64,128]{3,2,1,0:T(8,128)S(1)}, u32[]{:S(2)}, u32[]{:S(2)}) collective-permute-start(f32[1,32,64,128]{3,2,1,0:T(8,128)S(1)} %get-tuple-element.7), channel_id=1, source_target_pairs={{64,0},{65,1},{66,2},{67,3},{68,4},{69,5},{70,6},{71,7},{72,8},{73... | collective-permute-start | bytes 3145736 | tf_op jit(solution)/shard_map/ppermute | solution.py:20
  230.2 17.7 %collective-permute-start.20 = (f32[8,1,64,128]{3,2,1,0:T(8,128)S(1)}, f32[8,1,64,128]{3,2,1,0:T(8,128)}, u32[]{:S(2)}, u32[]{:S(2)}) collective-permute-start(f32[8,1,64,128]{3,2,1,0:T(8,128)S(1)} %get-tuple-element.8), channel_id=1, source_target_pairs={{0,8},{8,16},{16,24},{24,32},{32,40},{40,48},{48,56},{1,9},{9,17},... | collective-permute-start | bytes 786440 | tf_op jit(solution)/shard_map/ppermute | solution.py:19
  232.1 19.0 %collective-permute-start.21 = (f32[8,1,64,128]{3,2,1,0:T(8,128)}, f32[8,1,64,128]{3,2,1,0:T(8,128)S(1)}, u32[]{:S(2)}, u32[]{:S(2)}) collective-permute-start(f32[8,1,64,128]{3,2,1,0:T(8,128)} %get-tuple-element.9), channel_id=1, source_target_pairs={{8,0},{16,8},{24,16},{32,24},{40,32},{48,40},{56,48},{9,1},{17,9},... | collective-permute-start | bytes 786440 | tf_op jit(solution)/shard_map/ppermute | solution.py:20
  240.6 10.7 %collective-permute-start.23 = (f32[8,32,1,128]{3,1,2,0:T(8,128)}, f32[8,32,1,128]{3,1,2,0:T(8,128)S(1)}, u32[]{:S(2)}, u32[]{:S(2)}) collective-permute-start(f32[8,32,1,128]{3,1,2,0:T(8,128)} %bitcast.10), channel_id=1, source_target_pairs={{1,0},{2,1},{3,2},{4,3},{5,4},{6,5},{7,6},{9,8},{10,9},{11,10},{12... | collective-permute-start | bytes 393224 | tf_op jit(solution)/shard_map/ppermute | solution.py:20
  247.9 7.2 %collective-permute-start.22 = (f32[8,32,1,128]{3,1,2,0:T(8,128)}, f32[8,32,1,128]{3,1,2,0:T(8,128)}, u32[]{:S(2)}, u32[]{:S(2)}) collective-permute-start(f32[8,32,1,128]{3,1,2,0:T(8,128)} %bitcast.8), channel_id=1, source_target_pairs={{0,1},{1,2},{2,3},{3,4},{4,5},{5,6},{6,7},{8,9},{9,10},{10,11},{11... | collective-permute-start | bytes 393224 | tf_op jit(solution)/shard_map/ppermute | solution.py:19
where the time goes:
time: 326 us; the launch traced here: 323 us
  other arithmetic  133 us (41%)
  starting transfers between devices  80.7 us (25%)
  waiting for transfers between devices  55.5 us (17%)
  local copies, waits for them, and re-layouts  32 us (10%)
  blocking collectives  20.8 us (6%)
    add x4, other arithmetic, explicit_update(): return middle + scaled_diffusivity * spread + scaled_forcing  115 us
    ppermute x12, starting transfers between devices, with_halo(): lax.ppermute(last, axis, up)  42.4 us
    ppermute x12, waiting for transfers between devices, with_halo(): lax.ppermute(last, axis, up)  39 us
    ppermute x12, starting transfers between devices, with_halo(): lax.ppermute(initial, axis, [(b, a) for a, b in up])  38.3 us
    all_gather x3, blocking collectives, prefix_by_axis(): pieces = lax.all_gather(total, axis)  20.8 us
    slice x11, local copies, waits for them, and re-layouts, with_halo(): last = lax.slice_in_dim(x, length - width, length, axis=dim)  19.5 us
    ppermute x12, waiting for transfers between devices, with_halo(): lax.ppermute(initial, axis, [(b, a) for a, b in up])  16.5 us
    div x1, other arithmetic, per_device(): (present_layer + previous_plane) / (initial_state.shape[1] * lax.axis_siz...  8.81 us
  transfers between devices with their start and end apart: 24, of which 8 were waited for; matrix products, arithmetic and copies ran while one was open for 7% of the time, Pallas kernels for 0%

commit v1 on v0

v1 whole, which is shorter than its diff:
```python
import jax
import jax.numpy as jnp
from jax import lax
from jax.experimental import pallas as pl
from jax.experimental.pallas import tpu as pltpu
from jax.sharding import PartitionSpec as P

STEPS = 4
MESH = pl.DeviceIdType.MESH
Q, N, K, M = 8, 32, 64, 128
PAD = 8
TOP = PAD + K
CHUNKS = 8
ROWS = N // CHUNKS
ORDER = (0, 7, 1, 2, 3, 4, 5, 6)
WINDOW = 3
A, B = 0, 1
PLANES = ((0, Q - 1), (Q - 1, 1))


def exchange(x, d, f, last, before, s, dv, fv, lev_out, lev_in, tot, from_even, pair, from_odd, pair_before,
             in_sem, lat_s, lat_r, lon_s, lon_r, lev_s, lev_r, even_s, even_r, odd_s, odd_r, back_s, back_r):
    la, lo, le = lax.axis_index("lat"), lax.axis_index("lon"), lax.axis_index("lev")
    lon_size, lev_size = lax.axis_size("lon"), lax.axis_size("lev")
    has_lon = (lo > 0, lo < lon_size - 1)
    has_lev = (le > 0, le < lev_size - 1)
    odd = lo % 2 == 1
    slots = lon_size // 2

    def load(n, q):
        j = q + la * (Q - 1 - 2 * q)
        if n == 0:
            return pltpu.make_async_copy(x.at[j], s.at[0, q + 1, pl.ds(1, N), pl.ds(PAD, K), :], in_sem.at[0, q])
        return pltpu.make_async_copy((d, f)[n - 1].at[j], (dv, fv)[n - 1].at[q], in_sem.at[n, q])

    load(0, Q - 1).start()
    for q in range(Q - 1):
        load(0, q).start()
    for q in range(Q):
        load(1, q).start()
        load(2, q).start()

    barrier = pltpu.get_barrier_semaphore()

    def greet(dev):
        pl.semaphore_signal(barrier, inc=1, device_id=dev, device_id_type=MESH)

    greet((1 - la, lo, le))
    count = jnp.int32(1)
    peers = [
        (has_lon[0], (la, lo - 1, le)),
        (has_lon[1], (la, lo + 1, le)),
        (has_lev[0], (la, lo, le - 1)),
        (has_lev[1], (la, lo, le + 1)),
    ]
    for far in range(1, slots):
        peers.append((odd & (lo >= 2 * far), (la, lo - 2 * far, le)))
        peers.append((odd & (lo + 2 * far < lon_size), (la, lo + 2 * far, le)))
    for there, dev in peers:
        count = count + there.astype(jnp.int32)

        @pl.when(there)
        def _():
            greet(dev)

    zero_row = jnp.zeros((K, M), jnp.float32)
    zero_cell = jnp.zeros((1, M), jnp.float32)

    @pl.loop(0, N)
    def _(i):
        for b in range(2):
            s[b, 0, i + 1, pl.ds(PAD, K), :] = zero_row

    for side, row in ((0, 0), (1, N + 1)):
        @pl.when(jnp.logical_not(has_lon[side]))
        def _():
            @pl.loop(0, Q)
            def _(q):
                for b in range(2):
                    s[b, q + 1, row, pl.ds(PAD, K), :] = zero_row

    for side, cell in ((0, PAD - 1), (1, TOP)):
        @pl.when(jnp.logical_not(has_lev[side]))
        def _():
            @pl.loop(0, Q)
            def _(q):
                @pl.loop(0, N)
                def _(i):
                    for b in range(2):
                        s[b, q + 1, i + 1, pl.ds(cell, 1), :] = zero_cell

    pl.semaphore_wait(barrier, count)

    def lat_copy(tick):
        t, c = tick // CHUNKS, ORDER[tick % CHUNKS]
        rows = pl.ds(1 + c * ROWS, ROWS)
        return pltpu.make_async_remote_copy(
            src_ref=s.at[t % 2, Q, rows, pl.ds(PAD, K), :],
            dst_ref=s.at[t % 2, Q + 1, rows, pl.ds(PAD, K), :],
            send_sem=lat_s.at[tick], recv_sem=lat_r.at[tick],
            device_id=(1 - la, lo, le), device_id_type=MESH)

    def lon_copy(t, group, side):
        q0, n = PLANES[group]
        src, dst = ((1, N + 1), (N, 0))[side]
        planes = pl.ds(q0 + 1, n)
        return pltpu.make_async_remote_copy(
            src_ref=s.at[t % 2, planes, src, pl.ds(PAD, K), :],
            dst_ref=s.at[t % 2, planes, dst, pl.ds(PAD, K), :],
            send_sem=lon_s.at[t, group, side], recv_sem=lon_r.at[t, group, side],
            device_id=(la, lo + (-1, 1)[side], le), device_id_type=MESH)

    def lev_copy(t, group, side):
        q0, n = PLANES[group]
        planes = pl.ds(q0, n)
        return pltpu.make_async_remote_copy(
            src_ref=lev_out.at[t % 2, side, planes],
            dst_ref=lev_in.at[t, side, planes],
            send_sem=lev_s.at[t, group, side], recv_sem=lev_r.at[t, group, side],
            device_id=(la, lo, le + (-1, 1)[side]), device_id_type=MESH)

    def send_lon(t, group, side):
        @pl.when(has_lon[side])
        def _():
            lon_copy(t, group, side).start()

    def send_lev(t, group):
        q0, n = PLANES[group]

        @pl.loop(q0, q0 + n)
        def _(q):
            @pl.loop(0, N)
            def _(i):
                lev_out[t % 2, 0, q, i] = s[t % 2, q + 1, i + 1, pl.ds(PAD, 1), :]
                lev_out[t % 2, 1, q, i] = s[t % 2, q + 1, i + 1, pl.ds(TOP - 1, 1), :]

        for side in range(2):
            @pl.when(has_lev[side])
            def _():
                lev_copy(t, group, side).start()

    def sent(t, group):
        for side in range(2):
            @pl.when(has_lon[side])
            def _():
                lon_copy(t, group, side).wait_send()

            @pl.when(has_lev[side])
            def _():
                lev_copy(t, group, side).wait_send()

    def arrived(t, group):
        q0, n = PLANES[group]
        for side in range(2):
            @pl.when(has_lon[1 - side])
            def _():
                lon_copy(t, group, side).wait_recv()

            @pl.when(has_lev[1 - side])
            def _():
                lev_copy(t, group, side).wait_recv()
                cell = (TOP, PAD - 1)[side]

                @pl.loop(q0, q0 + n)
                def _(q):
                    @pl.loop(0, N)
                    def _(i):
                        s[t % 2, q + 1, i + 1, pl.ds(cell, 1), :] = lev_in[t, side, q, i]

    def update(t, q, i):
        b = t % 2
        here = s.at[b, q + 1, i + 1]
        middle = here[pl.ds(PAD, K), :]
        spread = here[pl.ds(PAD - 1, K), :] + here[pl.ds(PAD + 1, K), :]
        spread += s[b, q + 1, i, pl.ds(PAD, K), :] + s[b, q + 1, i + 2, pl.ds(PAD, K), :]
        spread += s[b, q, i + 1, pl.ds(PAD, K), :] + s[b, q + 2, i + 1, pl.ds(PAD, K), :]
        new = middle + dv[q, i] * (spread - 6.0 * middle) + fv[q, i]
        if t == STEPS - 1:
            last[q, i] = new
        else:
            s[1 - b, q + 1, i + 1, pl.ds(PAD, K), :] = new
        return new

    def update_group_a(t):
        @pl.loop(0, Q - 1)
        def _(q):
            if t == STEPS - 1:
                def row(i, total):
                    return total + update(t, q, i)
                tot[q] = lax.fori_loop(0, N, row, zero_row)
            else:
                @pl.loop(0, N)
                def _(i):
                    update(t, q, i)

    def update_chunk(t, c):
        if t == STEPS - 1:
            def row(i, total):
                return total + update(t, Q - 1, i)
            total = lax.fori_loop(c * ROWS, (c + 1) * ROWS, row, zero_row)
            if c == ORDER[0]:
                tot[Q - 1] = total
            else:
                tot[Q - 1] = tot[Q - 1] + total
        else:
            @pl.loop(c * ROWS, (c + 1) * ROWS)
            def _(i):
                update(t, Q - 1, i)

    def even_copy(group):
        planes = pl.ds(*PLANES[group])
        return pltpu.make_async_remote_copy(
            src_ref=tot.at[planes], dst_ref=from_even.at[planes],
            send_sem=even_s.at[group], recv_sem=even_r.at[group],
            device_id=(la, lo + 1, le), device_id_type=MESH)

    def odd_copy(group, far, slot):
        planes = pl.ds(*PLANES[group])
        return pltpu.make_async_remote_copy(
            src_ref=pair.at[planes], dst_ref=from_odd.at[slot, planes],
            send_sem=odd_s.at[group, far], recv_sem=odd_r.at[group, slot],
            device_id=(la, lo + 2 * far, le), device_id_type=MESH)

    def back_copy(group):
        planes = pl.ds(*PLANES[group])
        return pltpu.make_async_remote_copy(
            src_ref=pair_before.at[planes], dst_ref=before.at[planes],
            send_sem=back_s.at[group], recv_sem=back_r.at[group],
            device_id=(la, lo - 1, le), device_id_type=MESH)

    def prefix_0(group):
        @pl.when(jnp.logical_not(odd))
        def _():
            even_copy(group).start()

    def prefix_1(group):
        q0, n = PLANES[group]

        @pl.when(odd)
        def _():
            even_copy(group).wait_recv()
            @pl.loop(q0, q0 + n)
            def _(q):
                pair[q] = tot[q] + from_even[q]

            for far in range(1, slots):
                @pl.when(lo + 2 * far < lon_size)
                def _():
                    odd_copy(group, far, far - 1).start()

    def prefix_2(group):
        q0, n = PLANES[group]

        @pl.when(odd)
        def _():
            @pl.loop(q0, q0 + n)
            def _(q):
                pair_before[q] = zero_row

            for far in range(1, slots):
                @pl.when(lo >= 2 * far)
                def _():
                    odd_copy(group, far, far - 1).wait_recv()

                    @pl.loop(q0, q0 + n)
                    def _(q):
                        pair_before[q] = pair_before[q] + from_odd[far - 1, q]

            back_copy(group).start()

            @pl.loop(q0, q0 + n)
            def _(q):
                before[q] = pair_before[q] + from_even[q]

    def prefix_3(group):
        @pl.when(odd)
        def _():
            back_copy(group).wait_send()
            for far in range(1, slots):
                @pl.when(lo + 2 * far < lon_size)
                def _():
                    odd_copy(group, far, far - 1).wait_send()

        @pl.when(jnp.logical_not(odd))
        def _():
            back_copy(group).wait_recv()
            even_copy(group).wait_send()

    load(0, Q - 1).wait()
    for tick in range(WINDOW):
        lat_copy(tick).start()
    for side in range(2):
        send_lon(0, B, side)
    send_lev(0, B)
    for q in range(Q - 1):
        load(0, q).wait()
    for side in range(2):
        send_lon(0, A, side)
    send_lev(0, A)
    for q in range(Q):
        load(1, q).wait()
        load(2, q).wait()

    ticks = STEPS * CHUNKS
    for t in range(STEPS):
        final = t == STEPS - 1
        arrived(t, A)
        if t > 0:
            sent(t - 1, A)
        update_group_a(t)
        if final:
            prefix_0(A)
        else:
            for side in range(2):
                send_lon(t + 1, A, side)
            send_lev(t + 1, A)
        arrived(t, B)
        if t > 0:
            sent(t - 1, B)
        for n in range(CHUNKS):
            tick, c = t * CHUNKS + n, ORDER[n]
            lat_copy(tick).wait_recv()
            if t > 0:
                lat_copy(tick - CHUNKS).wait_send()
            update_chunk(t, c)
            if not final:
                if c == 0:
                    send_lon(t + 1, B, 0)
                if c == CHUNKS - 1:
                    send_lon(t + 1, B, 1)
            if tick + WINDOW < ticks:
                lat_copy(tick + WINDOW).start()
            if final and n == 1:
                prefix_1(A)
            if final and n == CHUNKS - 2:
                prefix_2(A)
        if not final:
            send_lev(t + 1, B)
    prefix_0(B)
    prefix_1(B)
    prefix_2(B)
    for n in range(CHUNKS):
        lat_copy(ticks - CHUNKS + n).wait_send()
    for group in (A, B):
        sent(STEPS - 1, group)
        prefix_3(group)


def finish(last, before, totals, end, run, t_sem, c_sem):
    la = lax.axis_index("lat")
    scale = 1.0 / (N * lax.axis_size("lon"))

    def place(q):
        return q + la * (Q - 1 - 2 * q)

    def put_end(q):
        return pltpu.make_async_copy(last.at[q], end.at[place(q)], t_sem.at[q])

    def put_totals(q):
        return pltpu.make_async_copy(run.at[q], totals.at[place(q)], c_sem.at[q])

    for q in range(Q):
        put_end(q).start()
    for q in range(Q):
        def row(i, total):
            total = total + last[q, i]
            run[q, i] = total * scale
            return total
        lax.fori_loop(0, N, row, before[q])
        put_totals(q).start()
    for q in range(Q):
        put_end(q).wait()
        put_totals(q).wait()


def per_device(x, d, f):
    hbm = pl.BlockSpec(memory_space=pltpu.HBM)
    vmem = pl.BlockSpec(memory_space=pltpu.VMEM)
    slots = lax.axis_size("lon") // 2
    dma = pltpu.SemaphoreType.DMA
    block = (Q, N, K, M)
    part = (Q, K, M)
    f32 = jnp.float32
    last, before = pl.pallas_call(
        exchange,
        out_shape=(pltpu.VMEM(block, f32), pltpu.VMEM(part, f32)),
        in_specs=[hbm] * 3,
        out_specs=(vmem, vmem),
        scratch_shapes=[
            pltpu.VMEM((2, Q + 2, N + 2, K + 2 * PAD, M), f32),
            pltpu.VMEM(block, f32),
            pltpu.VMEM(block, f32),
            pltpu.VMEM((2, 2, Q, N, 1, M), f32),
            pltpu.VMEM((STEPS, 2, Q, N, 1, M), f32),
            pltpu.VMEM(part, f32),
            pltpu.VMEM(part, f32),
            pltpu.VMEM(part, f32),
            pltpu.VMEM((slots - 1,) + part, f32),
            pltpu.VMEM(part, f32),
            dma((3, Q)),
            dma((STEPS * CHUNKS,)), dma((STEPS * CHUNKS,)),
            dma((STEPS, 2, 2)), dma((STEPS, 2, 2)),
            dma((STEPS, 2, 2)), dma((STEPS, 2, 2)),
            dma((2,)), dma((2,)),
            dma((2, slots)), dma((2, slots)),
            dma((2,)), dma((2,)),
        ],
        compiler_params=pltpu.CompilerParams(
            collective_id=0, has_side_effects=True, vmem_limit_bytes=52 * 1024 * 1024),
        name="exchange",
    )(x, d, f)
    totals, end = pl.pallas_call(
        finish,
        out_shape=(jax.ShapeDtypeStruct(block, f32), jax.ShapeDtypeStruct(block, f32)),
        in_specs=[vmem, vmem],
        out_specs=(hbm, hbm),
        scratch_shapes=[pltpu.VMEM(block, f32), dma((Q,)), dma((Q,))],
        compiler_params=pltpu.CompilerParams(vmem_limit_bytes=16 * 1024 * 1024),
        name="finish",
    )(last, before)
    return totals, end


def solution(mesh):
    spec = P("lat", "lon", "lev", None)
    return jax.shard_map(
        per_device, mesh=mesh, in_specs=(spec,) * 3, out_specs=(spec, spec), check_vma=False)
```

time: 326 us -> 146 us (0.45)
  Pallas kernels: 0 us -> 143 us
  other arithmetic: 133 us -> 0 us
  starting transfers between devices: 80.7 us -> 0 us
  waiting for transfers between devices: 55.5 us -> 0 us
  local copies, waits for them, and re-layouts: 32 us -> 0 us
  blocking collectives: 20.8 us -> 0 us
    pallas_call x0 -> x2, Pallas kernels: none -> 143 us  [the longest x1 137 us: per_device(): pl.pallas_call(exchange, out_shape=(pltpu.VMEM(block, f32), pltpu.VMEM(pa...]
    add x7 -> x0, other arithmetic: 115 us -> none  [the longest x4 115 us: explicit_update(): return middle + scaled_diffusivity * spread + scaled_forcing]
    ppermute x24 -> x0, starting transfers between devices: 80.7 us -> none  [the longest x12 42.4 us: with_halo(): lax.ppermute(last, axis, up)]
    ppermute x24 -> x0, waiting for transfers between devices: 55.5 us -> none  [the longest x12 39 us: with_halo(): lax.ppermute(last, axis, up)]
    slice x13 -> x0, local copies, waits for them, and re-layouts: 22.3 us -> none  [the longest x11 19.5 us: with_halo(): last = lax.slice_in_dim(x, length - width, length, axis=dim)]
    all_gather x3 -> x0, blocking collectives: 20.8 us -> none  [prefix_by_axis(): pieces = lax.all_gather(total, axis)]
    div x1 -> x0, other arithmetic: 8.81 us -> none  [per_device(): (present_layer + previous_plane) / (initial_state.shape[1] * lax.axis_siz...]
    another operation x1 -> x0, other arithmetic: 8.42 us -> none  [per_device(): present_layer = jnp.cumsum(initial_state, axis=1)]
  transfers between devices with their start and end apart: 24 -> 0, of which waited for: 8 -> 0; matrix products, arithmetic and copies ran while one was open for 7% -> 0% of each run, Pallas kernels for 0% -> 0%
where the time goes in v1:
time: 146 us; the launch traced here: 144 us
  Pallas kernels  143 us (98%)
    pallas_call x1, Pallas kernels, per_device(): pl.pallas_call(exchange, out_shape=(pltpu.VMEM(block, f32), pltpu.VMEM(pa...  137 us
    pallas_call x1, Pallas kernels, per_device(): pl.pallas_call(finish, out_shape=(jax.ShapeDtypeStruct(block, f32), jax.S...  5.97 us

profile of v1, /device:TPU:56, one launch (start us, length us, event | category | flops | bytes accessed | tf_op | source)
XLA Modules:
  0.0 143.7 jit_solution(7384873474100653542)
XLA Ops:
  0.6 137.1 %exchange.1 = (f32[8,32,64,128]{3,2,1,0:T(8,128)S(1)}, f32[8,64,128]{2,1,0:T(8,128)S(1)}) custom-call(f32[8,32,64,128]{3,2,1,0:T(8,128)} %x.1, f32[8,32,64,128]{3,2,1,0:T(8,128)} %d.1, f32[8,32,64,128]{3,2,1,0:T(8,128)} %f.1), custom_call_target="tpu_custom_call" | custom-call | tf_op jit(solution)/shard_map/exchange/pallas_call | solution.py:384
  137.7 6.0 %finish.1 = (f32[8,32,64,128]{3,2,1,0:T(8,128)}, f32[8,32,64,128]{3,2,1,0:T(8,128)}) custom-call(f32[8,32,64,128]{3,2,1,0:T(8,128)S(1)} %get-tuple-element.4.last, f32[8,64,128]{2,1,0:T(8,128)S(1)} %get-tuple-element.5.before), custom_call_target="tpu_custom_call" | custom-call | tf_op jit(solution)/shard_map/finish/pallas_call | solution.py:412

commit v2 on v1

v2 whole, which is shorter than its diff:
```python
import jax
import jax.numpy as jnp
from jax import lax
from jax.experimental import pallas as pl
from jax.experimental.pallas import tpu as pltpu
from jax.sharding import PartitionSpec as P

STEPS = 4
MESH = pl.DeviceIdType.MESH
Q, N, K, M = 8, 32, 64, 128
PAD = 8
TOP = PAD + K
EDGE = Q - 1
CHUNKS = 8
ROWS = N // CHUNKS
ORDER = (0, 7, 1, 2, 3, 4, 5, 6)
WINDOW = 4
TICKS = STEPS * CHUNKS
RELAY = (2, 4, 6)
LATE = {2: (2, 0), 3: (3, 1), 4: (4,), 5: (5,), 6: (6,), 7: (7,)}
A, B = 0, 1
PLANES = ((0, Q - 1), (Q - 1, 1))


def exchange(x, d, f, last, before, s, dv, fv, hold, tot, from_even, pair, from_odd, pair_before,
             in_sem, lat_s, lat_r, lon_s, lon_r, lev_s, lev_r, hold_s, hold_r, turn_s,
             even_s, even_r, odd_s, odd_r, back_s, back_r):
    la, lo, le = lax.axis_index("lat"), lax.axis_index("lon"), lax.axis_index("lev")
    lon_size, lev_size = lax.axis_size("lon"), lax.axis_size("lev")
    half = lon_size // 2
    has_lon = (lo > 0, lo < lon_size - 1)
    has_lev = (le > 0, le < lev_size - 1)
    odd = lo % 2 == 1
    even = lo % 2 == 0
    near = (odd, even)
    wide = (even & (lo > 0), odd & (lo < lon_size - 1))
    slots = lon_size // 2
    cells = pl.ds(PAD, K)

    def load(n, q):
        j = q + la * (Q - 1 - 2 * q)
        if n == 0:
            return pltpu.make_async_copy(x.at[j], s.at[0, q + 1, pl.ds(1, N), cells, :], in_sem.at[0, q])
        return pltpu.make_async_copy((d, f)[n - 1].at[j], (dv, fv)[n - 1].at[q], in_sem.at[n, q])

    load(0, EDGE).start()
    for q in range(EDGE):
        load(0, q).start()

    barrier = pltpu.get_barrier_semaphore()

    def greet(dev):
        pl.semaphore_signal(barrier, inc=1, device_id=dev, device_id_type=MESH)

    greet((1 - la, lo, le))
    count = jnp.int32(1)
    peers = [
        (has_lon[0], (la, lo - 1, le)),
        (has_lon[1], (la, lo + 1, le)),
        (has_lev[0], (la, lo, le - 1)),
        (has_lev[1], (la, lo, le + 1)),
        (wide[0], (1 - la, lo - 1, le)),
        (wide[1], (1 - la, lo + 1, le)),
        (lo == 0, (la, half, le)),
        (lo == half, (la, 0, le)),
        (lo == 0, (la, half - 1, le)),
        (lo == half - 1, (la, 0, le)),
        (lo == lon_size - 1, (la, half, le)),
        (lo == half, (la, lon_size - 1, le)),
    ]
    for far in range(1, slots):
        peers.append((odd & (lo >= 2 * far), (la, lo - 2 * far, le)))
        peers.append((odd & (lo + 2 * far < lon_size), (la, lo + 2 * far, le)))
    for there, dev in peers:
        count = count + there.astype(jnp.int32)

        @pl.when(there)
        def _():
            greet(dev)

    zero_row = jnp.zeros((K, M), jnp.float32)
    zero_cell = jnp.zeros((1, M), jnp.float32)

    @pl.loop(0, N)
    def _(i):
        for b in range(2):
            s[b, 0, i + 1, cells, :] = zero_row

    for side, row in ((0, 0), (1, N + 1)):
        @pl.when(jnp.logical_not(has_lon[side]))
        def _():
            @pl.loop(0, Q)
            def _(q):
                for b in range(2):
                    s[b, q + 1, row, cells, :] = zero_row

    for side, cell in ((0, PAD - 1), (1, TOP)):
        @pl.when(jnp.logical_not(has_lev[side]))
        def _():
            @pl.loop(0, Q)
            def _(q):
                @pl.loop(0, N)
                def _(i):
                    for b in range(2):
                        s[b, q + 1, i + 1, pl.ds(cell, 1), :] = zero_cell

    pl.semaphore_wait(barrier, count)

    def lat_copy(tick):
        t, c = tick // CHUNKS, ORDER[tick % CHUNKS]
        rows = pl.ds(1 + c * ROWS, ROWS)
        return pltpu.make_async_remote_copy(
            src_ref=s.at[t % 2, Q, rows, cells, :],
            dst_ref=s.at[t % 2, Q + 1, rows, cells, :],
            send_sem=lat_s.at[tick], recv_sem=lat_r.at[tick],
            device_id=(1 - la, lo, le), device_id_type=MESH)

    FROM, TO = (1, N), (N + 1, 0)

    def lon_copy(t, q, side):
        return pltpu.make_async_remote_copy(
            src_ref=s.at[t % 2, q + 1, FROM[side], cells, :],
            dst_ref=s.at[t % 2, q + 1, TO[side], cells, :],
            send_sem=lon_s.at[t, q, side], recv_sem=lon_r.at[t, q, side],
            device_id=(la, lo + (-1, 1)[side], le), device_id_type=MESH)

    def hold_copy(t, q, side):
        r = RELAY.index(q)
        return pltpu.make_async_remote_copy(
            src_ref=s.at[t % 2, q + 1, FROM[side], cells, :],
            dst_ref=hold.at[t, r],
            send_sem=lon_s.at[t, q, side], recv_sem=hold_r.at[t, r],
            device_id=(la, lo + (-half, half)[side], le), device_id_type=MESH)

    def pass_copy(t, q, side):
        r = RELAY.index(q)
        return pltpu.make_async_remote_copy(
            src_ref=hold.at[t, r],
            dst_ref=s.at[t % 2, q + 1, TO[side], cells, :],
            send_sem=hold_s.at[t, r], recv_sem=lon_r.at[t, q, side],
            device_id=(la, lo + (half - 1, 1 - half)[side], le), device_id_type=MESH)

    def turn_copy(t, side):
        return pltpu.make_async_remote_copy(
            src_ref=s.at[t % 2, Q + 1, FROM[side], cells, :],
            dst_ref=s.at[t % 2, Q, TO[side], cells, :],
            send_sem=turn_s.at[t], recv_sem=lon_r.at[t, EDGE, side],
            device_id=(1 - la, lo + (-1, 1)[side], le), device_id_type=MESH)

    def lev_copy(t, q, side):
        return pltpu.make_async_remote_copy(
            src_ref=s.at[t % 2, q + 1, pl.ds(1, N), pl.ds((PAD, TOP - 1)[side], 1), :],
            dst_ref=s.at[t % 2, q + 1, pl.ds(1, N), pl.ds((TOP, PAD - 1)[side], 1), :],
            send_sem=lev_s.at[t, q, side], recv_sem=lev_r.at[t, q, side],
            device_id=(la, lo, le + (-1, 1)[side]), device_id_type=MESH)

    sender = (lo == half, lo == half - 1)
    keeper = (lo == 0, lo == lon_size - 1)

    def send_lev(t, q):
        for side in range(2):
            @pl.when(has_lev[side])
            def _():
                lev_copy(t, q, side).start()

    def send_lon(t, q):
        for side in range(2):
            if q in RELAY:
                @pl.when(has_lon[side] & jnp.logical_not(sender[side]))
                def _():
                    lon_copy(t, q, side).start()

                @pl.when(sender[side])
                def _():
                    hold_copy(t, q, side).start()
            else:
                @pl.when(has_lon[side])
                def _():
                    lon_copy(t, q, side).start()

    def send_near(t, side):
        @pl.when(near[side])
        def _():
            lon_copy(t, EDGE, side).start()

    def pass_on(t, q):
        for side in range(2):
            @pl.when(keeper[side])
            def _():
                hold_copy(t, q, side).wait_recv()
                pass_copy(t, q, side).start()

    def sent_lev(t, q):
        for side in range(2):
            @pl.when(has_lev[side])
            def _():
                lev_copy(t, q, side).wait_send()

    def sent_lon(t, q):
        for side in range(2):
            @pl.when(near[side] if q == EDGE else has_lon[side])
            def _():
                lon_copy(t, q, side).wait_send()

    def arrived_lev(t, q):
        for side in range(2):
            @pl.when(has_lev[1 - side])
            def _():
                lev_copy(t, q, side).wait_recv()

    def arrived_lon(t, q, side):
        @pl.when(has_lon[1 - side])
        def _():
            lon_copy(t, q, side).wait_recv()

    def update(t, q, i):
        b = t % 2
        here = s.at[b, q + 1, i + 1]
        middle = here[cells, :]
        spread = here[pl.ds(PAD - 1, K), :] + here[pl.ds(PAD + 1, K), :]
        spread += s[b, q + 1, i, cells, :] + s[b, q + 1, i + 2, cells, :]
        spread += s[b, q, i + 1, cells, :] + s[b, q + 2, i + 1, cells, :]
        new = middle + dv[q, i] * (spread - 6.0 * middle) + fv[q, i]
        if t == STEPS - 1:
            last[q, i] = new
        else:
            s[1 - b, q + 1, i + 1, cells, :] = new
        return new

    def update_plane(t, q):
        if t == STEPS - 1:
            def row(i, total):
                return total + update(t, q, i)
            tot[q] = lax.fori_loop(0, N, row, zero_row)
        else:
            @pl.loop(0, N)
            def _(i):
                update(t, q, i)

    def update_chunk(t, n):
        c = ORDER[n]
        if t == STEPS - 1:
            def row(i, total):
                return total + update(t, EDGE, i)
            total = lax.fori_loop(c * ROWS, (c + 1) * ROWS, row, zero_row)
            if n == LATE[2][0]:
                tot[EDGE] = total
            else:
                tot[EDGE] = tot[EDGE] + total
        else:
            @pl.loop(c * ROWS, (c + 1) * ROWS)
            def _(i):
                update(t, EDGE, i)

    def even_copy(group):
        planes = pl.ds(*PLANES[group])
        return pltpu.make_async_remote_copy(
            src_ref=tot.at[planes], dst_ref=from_even.at[planes],
            send_sem=even_s.at[group], recv_sem=even_r.at[group],
            device_id=(la, lo + 1, le), device_id_type=MESH)

    def odd_copy(group, far, slot):
        planes = pl.ds(*PLANES[group])
        return pltpu.make_async_remote_copy(
            src_ref=pair.at[planes], dst_ref=from_odd.at[slot, planes],
            send_sem=odd_s.at[group, far], recv_sem=odd_r.at[group, slot],
            device_id=(la, lo + 2 * far, le), device_id_type=MESH)

    def back_copy(group):
        planes = pl.ds(*PLANES[group])
        return pltpu.make_async_remote_copy(
            src_ref=pair_before.at[planes], dst_ref=before.at[planes],
            send_sem=back_s.at[group], recv_sem=back_r.at[group],
            device_id=(la, lo - 1, le), device_id_type=MESH)

    def prefix_0(group):
        @pl.when(jnp.logical_not(odd))
        def _():
            even_copy(group).start()

    def prefix_1(group):
        q0, n = PLANES[group]

        @pl.when(odd)
        def _():
            even_copy(group).wait_recv()
            @pl.loop(q0, q0 + n)
            def _(q):
                pair[q] = tot[q] + from_even[q]

            for far in range(1, slots):
                @pl.when(lo + 2 * far < lon_size)
                def _():
                    odd_copy(group, far, far - 1).start()

    def prefix_2(group):
        q0, n = PLANES[group]

        @pl.when(odd)
        def _():
            @pl.loop(q0, q0 + n)
            def _(q):
                pair_before[q] = zero_row

            for far in range(1, slots):
                @pl.when(lo >= 2 * far)
                def _():
                    odd_copy(group, far, far - 1).wait_recv()

                    @pl.loop(q0, q0 + n)
                    def _(q):
                        pair_before[q] = pair_before[q] + from_odd[far - 1, q]

            back_copy(group).start()

            @pl.loop(q0, q0 + n)
            def _(q):
                before[q] = pair_before[q] + from_even[q]

    def prefix_3(group):
        @pl.when(odd)
        def _():
            back_copy(group).wait_send()
            for far in range(1, slots):
                @pl.when(lo + 2 * far < lon_size)
                def _():
                    odd_copy(group, far, far - 1).wait_send()

        @pl.when(jnp.logical_not(odd))
        def _():
            back_copy(group).wait_recv()
            even_copy(group).wait_send()

    load(0, EDGE).wait()
    lat_copy(0).start()
    for q in (0, 1, EDGE, 2, 3, 4, 5, 6):
        load(1, q).start()
        load(2, q).start()
    send_lev(0, EDGE)
    for side in range(2):
        send_near(0, side)
    for q in range(EDGE):
        load(0, q).wait()
    lat_copy(1).start()
    for q in range(EDGE):
        send_lev(0, q)
        send_lon(0, q)
        if q in (2, 4):
            lat_copy(q // 2 + 1).start()
    for tick in range(4, WINDOW):
        lat_copy(tick).start()

    for t in range(STEPS):
        final = t == STEPS - 1
        for n in range(CHUNKS):
            tick = t * CHUNKS + n
            lat_copy(tick).wait_recv()
            if tick + WINDOW < TICKS:
                lat_copy(tick + WINDOW).start()
            if n < 2:
                @pl.when(wide[n])
                def _():
                    turn_copy(t, n).start()
            if t == 0 and n + 2 in RELAY:
                pass_on(0, n + 2)
            if not final and n - 1 in RELAY:
                pass_on(t + 1, n - 1)
            for m in LATE.get(n, ()):
                if t == 0 and n == 2 and m == n:
                    load(1, EDGE).wait()
                    load(2, EDGE).wait()
                if m == 2:
                    arrived_lev(t, EDGE)
                    if t > 0:
                        sent_lev(t - 1, EDGE)
                        sent_lon(t - 1, EDGE)
                if m < 2:
                    arrived_lon(t, EDGE, 1 - m)

                    @pl.when(wide[m])
                    def _():
                        turn_copy(t, m).wait_send()
                if t > 0:
                    lat_copy(tick - n + m - CHUNKS).wait_send()
                update_chunk(t, m)
                if not final and m < 2:
                    send_near(t + 1, m)
            planes = ((n,) if n < EDGE else ()) if not final else tuple(q for q in (2 * n, 2 * n + 1) if q < EDGE)
            for q in planes:
                if t == 0:
                    load(1, q).wait()
                    load(2, q).wait()
                arrived_lev(t, q)
                for side in range(2):
                    arrived_lon(t, q, side)
                if t > 0:
                    sent_lev(t - 1, q)
                    sent_lon(t - 1, q)
                update_plane(t, q)
                if not final:
                    send_lev(t + 1, q)
                    send_lon(t + 1, q)
            if final and n == 3:
                prefix_0(A)
            if final and n == 4:
                prefix_1(A)
        if not final:
            send_lev(t + 1, EDGE)
    prefix_0(B)
    prefix_1(B)
    prefix_2(A)
    prefix_2(B)
    for n in range(CHUNKS):
        lat_copy(TICKS - CHUNKS + n).wait_send()
    for q in range(Q):
        sent_lev(STEPS - 1, q)
        sent_lon(STEPS - 1, q)
    for t in range(STEPS):
        for q in RELAY:
            for side in range(2):
                @pl.when(keeper[side])
                def _():
                    pass_copy(t, q, side).wait_send()
    for group in (A, B):
        prefix_3(group)


def finish(last, before, totals, end, run, t_sem, c_sem):
    la = lax.axis_index("lat")
    scale = 1.0 / (N * lax.axis_size("lon"))

    def place(q):
        return q + la * (Q - 1 - 2 * q)

    def put_end(q):
        return pltpu.make_async_copy(last.at[q], end.at[place(q)], t_sem.at[q])

    def put_totals(q):
        return pltpu.make_async_copy(run.at[q], totals.at[place(q)], c_sem.at[q])

    for q in range(Q):
        put_end(q).start()
    for q in range(Q):
        def row(i, total):
            total = total + last[q, i]
            run[q, i] = total * scale
            return total
        lax.fori_loop(0, N, row, before[q])
        put_totals(q).start()
    for q in range(Q):
        put_end(q).wait()
        put_totals(q).wait()


def per_device(x, d, f):
    hbm = pl.BlockSpec(memory_space=pltpu.HBM)
    vmem = pl.BlockSpec(memory_space=pltpu.VMEM)
    slots = lax.axis_size("lon") // 2
    dma = pltpu.SemaphoreType.DMA
    block = (Q, N, K, M)
    part = (Q, K, M)
    f32 = jnp.float32
    last, before = pl.pallas_call(
        exchange,
        out_shape=(pltpu.VMEM(block, f32), pltpu.VMEM(part, f32)),
        in_specs=[hbm] * 3,
        out_specs=(vmem, vmem),
        scratch_shapes=[
            pltpu.VMEM((2, Q + 2, N + 2, K + 2 * PAD, M), f32),
            pltpu.VMEM(block, f32),
            pltpu.VMEM(block, f32),
            pltpu.VMEM((STEPS, len(RELAY), K, M), f32),
            pltpu.VMEM(part, f32),
            pltpu.VMEM(part, f32),
            pltpu.VMEM(part, f32),
            pltpu.VMEM((slots - 1,) + part, f32),
            pltpu.VMEM(part, f32),
            dma((3, Q)),
            dma((TICKS,)), dma((TICKS,)),
            dma((STEPS, Q, 2)), dma((STEPS, Q, 2)),
            dma((STEPS, Q, 2)), dma((STEPS, Q, 2)),
            dma((STEPS, len(RELAY))), dma((STEPS, len(RELAY))), dma((STEPS,)),
            dma((2,)), dma((2,)),
            dma((2, slots)), dma((2, slots)),
            dma((2,)), dma((2,)),
        ],
        compiler_params=pltpu.CompilerParams(
            collective_id=0, has_side_effects=True, vmem_limit_bytes=52 * 1024 * 1024),
        name="exchange",
    )(x, d, f)
    totals, end = pl.pallas_call(
        finish,
        out_shape=(jax.ShapeDtypeStruct(block, f32), jax.ShapeDtypeStruct(block, f32)),
        in_specs=[vmem, vmem],
        out_specs=(hbm, hbm),
        scratch_shapes=[pltpu.VMEM(block, f32), dma((Q,)), dma((Q,))],
        compiler_params=pltpu.CompilerParams(vmem_limit_bytes=16 * 1024 * 1024),
        name="finish",
    )(last, before)
    return totals, end


def solution(mesh):
    spec = P("lat", "lon", "lev", None)
    return jax.shard_map(
        per_device, mesh=mesh, in_specs=(spec,) * 3, out_specs=(spec, spec), check_vma=False)
```

time: 146 us -> 129 us (0.88)
  Pallas kernels: 143 us -> 127 us
    pallas_call x1, Pallas kernels: 137 us -> 122 us  [per_device(): pl.pallas_call(exchange, out_shape=(pltpu.VMEM(block, f32), pltpu.VMEM(pa...]
where the time goes in v2:
time: 129 us; the launch traced here: 128 us
  Pallas kernels  127 us (98%)
    pallas_call x1, Pallas kernels, per_device(): pl.pallas_call(exchange, out_shape=(pltpu.VMEM(block, f32), pltpu.VMEM(pa...  122 us
    pallas_call x1, Pallas kernels, per_device(): pl.pallas_call(finish, out_shape=(jax.ShapeDtypeStruct(block, f32), jax.S...  5.97 us

profile of v2, /device:TPU:56, one launch (start us, length us, event | category | flops | bytes accessed | tf_op | source)
XLA Modules:
  0.0 128.1 jit_solution(10721512798153336985)
XLA Ops:
  0.6 121.5 %exchange.1 = (f32[8,32,64,128]{3,2,1,0:T(8,128)S(1)}, f32[8,64,128]{2,1,0:T(8,128)S(1)}) custom-call(f32[8,32,64,128]{3,2,1,0:T(8,128)} %x.1, f32[8,32,64,128]{3,2,1,0:T(8,128)} %d.1, f32[8,32,64,128]{3,2,1,0:T(8,128)} %f.1), custom_call_target="tpu_custom_call" | custom-call | tf_op jit(solution)/shard_map/exchange/pallas_call | solution.py:463
  122.1 6.0 %finish.1 = (f32[8,32,64,128]{3,2,1,0:T(8,128)}, f32[8,32,64,128]{3,2,1,0:T(8,128)}) custom-call(f32[8,32,64,128]{3,2,1,0:T(8,128)S(1)} %get-tuple-element.4.last, f32[8,64,128]{2,1,0:T(8,128)S(1)} %get-tuple-element.5.before), custom_call_target="tpu_custom_call" | custom-call | tf_op jit(solution)/shard_map/finish/pallas_call | solution.py:491

commit v3 on v2

v3 whole, which is shorter than its diff:
```python
import jax
import jax.numpy as jnp
from jax import lax
from jax.experimental import pallas as pl
from jax.experimental.pallas import tpu as pltpu
from jax.sharding import PartitionSpec as P

STEPS = 4
MESH = pl.DeviceIdType.MESH
Q, N, K, M = 8, 32, 64, 128
PAD = 8
TOP = PAD + K
EDGE = Q - 1
CHUNKS = 8
ROWS = N // CHUNKS
ORDER = (0, 7, 1, 2, 3, 4, 5, 6)
WINDOW = 4
TICKS = STEPS * CHUNKS
GROUPS = ((0, 2), (2, 2), (4, 2), (6, 1), (7, 1))
LAST = len(GROUPS) - 1
RELAY = (1, 3)
LATE = {2: (2, 0), 3: (3, 1), 4: (4,), 5: (5,), 6: (6,), 7: (7,)}
PIECES = 4
A, B = 0, 1
PLANES = ((0, Q - 1), (Q - 1, 1))
GREET = ((1, range(7)), (2, (0, 1, 3, 4, 5)), (3, (0, 1, 3, 4)), (4, (0, 1, 2, 3)), (5, (1,)), (6, (1,)))


def exchange(x, d, f, last, before, s, dv, fv, hold, tot, mate, pair, joint, over_z, over_x, through, earlier,
             in_sem, pair_sem, lat_s, lat_r, lon_s, lon_r, lev_s, lev_r, hold_s, hold_r, turn_s,
             mate_s, mate_r, z_s, z_r, x_s, x_r, back_s, back_r, far_s, far_r):
    la, lo, le = lax.axis_index("lat"), lax.axis_index("lon"), lax.axis_index("lev")
    lon_size, lev_size = lax.axis_size("lon"), lax.axis_size("lev")
    half = lon_size // 2
    has_lon = (lo > 0, lo < lon_size - 1)
    has_lev = (le > 0, le < lev_size - 1)
    odd = lo % 2 == 1
    even = lo % 2 == 0
    near = (odd, even)
    wide = (even & (lo > 0), odd & (lo < lon_size - 1))
    slots = lon_size // 2
    cells = pl.ds(PAD, K)

    def place(q):
        return q + la * (Q - 1 - 2 * q)

    def load(q):
        return pltpu.make_async_copy(x.at[place(q)], s.at[0, q + 1, pl.ds(1, N), cells, :], in_sem.at[q])

    def load_pair(n, p):
        planes = pl.ds(2 * p + la * (Q - 2 - 4 * p), 2)
        return pltpu.make_async_copy((d, f)[n - 1].at[planes], (dv, fv)[n - 1].at[planes], pair_sem.at[n - 1, p])

    load(EDGE).start()

    barrier = pltpu.get_barrier_semaphore()

    def greet(dev):
        pl.semaphore_signal(barrier, inc=1, device_id=dev, device_id_type=MESH)

    def among(members):
        found = lo < 0
        for m in members:
            found = found | (lo == m)
        return found

    greet((1 - la, lo, le))
    count = jnp.int32(1)
    peers = [
        (has_lev[0], (la, lo, le - 1)),
        (has_lev[1], (la, lo, le + 1)),
        (wide[0], (1 - la, lo - 1, le)),
        (wide[1], (1 - la, lo + 1, le)),
    ]
    for offset, lower in GREET:
        peers.append((among(lower), (la, lo + offset, le)))
        peers.append((among([m + offset for m in lower]), (la, lo - offset, le)))
    for there, dev in peers:
        count = count + there.astype(jnp.int32)

        @pl.when(there)
        def _():
            greet(dev)

    for q in range(EDGE):
        load(q).start()
    pl.semaphore_wait(barrier, count)

    zero_row = jnp.zeros((K, M), jnp.float32)
    zero_cell = jnp.zeros((1, M), jnp.float32)

    def lat_copy(tick):
        t, c = tick // CHUNKS, ORDER[tick % CHUNKS]
        rows = pl.ds(1 + c * ROWS, ROWS)
        return pltpu.make_async_remote_copy(
            src_ref=s.at[t % 2, Q, rows, cells, :],
            dst_ref=s.at[t % 2, Q + 1, rows, cells, :],
            send_sem=lat_s.at[tick % CHUNKS], recv_sem=lat_r.at[tick % CHUNKS],
            device_id=(1 - la, lo, le), device_id_type=MESH)

    FROM, TO = (1, N), (N + 1, 0)

    def face(t, g, i):
        q, n = GROUPS[g]
        return s.at[t % 2, pl.ds(q + 1, n), i, cells, :]

    def lon_copy(t, g, side):
        return pltpu.make_async_remote_copy(
            src_ref=face(t, g, FROM[side]), dst_ref=face(t, g, TO[side]),
            send_sem=lon_s.at[t % 2, g, side], recv_sem=lon_r.at[t % 2, g, side],
            device_id=(la, lo + (-1, 1)[side], le), device_id_type=MESH)

    def held(t, g):
        r = RELAY.index(g)
        return hold.at[t, pl.ds(2 * r, GROUPS[g][1])], t % 2, r

    def hold_copy(t, g, side):
        buffer, b, r = held(t, g)
        return pltpu.make_async_remote_copy(
            src_ref=face(t, g, FROM[side]), dst_ref=buffer,
            send_sem=lon_s.at[b, g, side], recv_sem=hold_r.at[b, r],
            device_id=(la, lo + (-half, half)[side], le), device_id_type=MESH)

    def pass_copy(t, g, side):
        buffer, b, r = held(t, g)
        return pltpu.make_async_remote_copy(
            src_ref=buffer, dst_ref=face(t, g, TO[side]),
            send_sem=hold_s.at[b, r], recv_sem=lon_r.at[b, g, side],
            device_id=(la, lo + (half - 1, 1 - half)[side], le), device_id_type=MESH)

    def turn_copy(t, side):
        return pltpu.make_async_remote_copy(
            src_ref=s.at[t % 2, Q + 1, FROM[side], cells, :],
            dst_ref=s.at[t % 2, Q, TO[side], cells, :],
            send_sem=turn_s, recv_sem=lon_r.at[t % 2, LAST, side],
            device_id=(1 - la, lo + (-1, 1)[side], le), device_id_type=MESH)

    def lev_copy(t, g, side):
        q, n = GROUPS[g]
        planes = pl.ds(q + 1, n)
        return pltpu.make_async_remote_copy(
            src_ref=s.at[t % 2, planes, pl.ds(1, N), pl.ds((PAD, TOP - 1)[side], 1), :],
            dst_ref=s.at[t % 2, planes, pl.ds(1, N), pl.ds((TOP, PAD - 1)[side], 1), :],
            send_sem=lev_s.at[t % 2, g, side], recv_sem=lev_r.at[t % 2, g, side],
            device_id=(la, lo, le + (-1, 1)[side]), device_id_type=MESH)

    sender = (lo == half, lo == half - 1)
    keeper = (lo == 0, lo == lon_size - 1)

    def send_lev(t, q):
        for side in range(2):
            @pl.when(has_lev[side])
            def _():
                lev_copy(t, q, side).start()

    def send_lon(t, q):
        for side in range(2):
            if q in RELAY:
                @pl.when(has_lon[side] & jnp.logical_not(sender[side]))
                def _():
                    lon_copy(t, q, side).start()

                @pl.when(sender[side])
                def _():
                    hold_copy(t, q, side).start()
            else:
                @pl.when(has_lon[side])
                def _():
                    lon_copy(t, q, side).start()

    def send_near(t, side):
        @pl.when(near[side])
        def _():
            lon_copy(t, LAST, side).start()

    def pass_on(t, q):
        for side in range(2):
            @pl.when(keeper[side])
            def _():
                if t > 1:
                    pass_copy(t - 2, q, side).wait_send()
                hold_copy(t, q, side).wait_recv()
                pass_copy(t, q, side).start()

    def sent_lev(t, q):
        for side in range(2):
            @pl.when(has_lev[side])
            def _():
                lev_copy(t, q, side).wait_send()

    def sent_lon(t, q):
        for side in range(2):
            @pl.when(near[side] if q == LAST else has_lon[side])
            def _():
                lon_copy(t, q, side).wait_send()

    def arrived_lev(t, q):
        for side in range(2):
            @pl.when(has_lev[1 - side])
            def _():
                lev_copy(t, q, side).wait_recv()

    def arrived_lon(t, q, side):
        @pl.when(has_lon[1 - side])
        def _():
            lon_copy(t, q, side).wait_recv()

    def update(t, q, i):
        b = t % 2
        here = s.at[b, q + 1, i + 1]
        middle = here[cells, :]
        spread = here[pl.ds(PAD - 1, K), :] + here[pl.ds(PAD + 1, K), :]
        spread += s[b, q + 1, i, cells, :] + s[b, q + 1, i + 2, cells, :]
        spread += s[b, q, i + 1, cells, :] + s[b, q + 2, i + 1, cells, :]
        j = place(q)
        new = middle + dv[j, i] * (spread - 6.0 * middle) + fv[j, i]
        if t == STEPS - 1:
            last[j, i] = new
        else:
            s[1 - b, q + 1, i + 1, cells, :] = new
        return new

    def update_plane(t, q):
        if t == STEPS - 1:
            def add(i, total):
                return total + update(t, q, i)
            tot[q] = lax.fori_loop(0, N, add, zero_row)
        else:
            @pl.loop(0, N)
            def _(i):
                update(t, q, i)

    def update_chunk(t, n):
        c = ORDER[n]
        if t == STEPS - 1:
            def add(i, total):
                return total + update(t, EDGE, i)
            total = lax.fori_loop(c * ROWS, (c + 1) * ROWS, add, zero_row)
            if n == LATE[2][0]:
                tot[EDGE] = total
            else:
                tot[EDGE] = tot[EDGE] + total
        else:
            @pl.loop(c * ROWS, (c + 1) * ROWS)
            def _(i):
                update(t, EDGE, i)

    def mate_copy(group):
        planes = pl.ds(*PLANES[group])
        return pltpu.make_async_remote_copy(
            src_ref=tot.at[planes], dst_ref=mate.at[planes],
            send_sem=mate_s.at[group], recv_sem=mate_r.at[group],
            device_id=(la, lo + (-1, 1)[group], le), device_id_type=MESH)

    rest = pl.ds(*PLANES[A])

    def z_copy():
        return pltpu.make_async_remote_copy(
            src_ref=pair, dst_ref=over_z, send_sem=z_s, recv_sem=z_r,
            device_id=(la, lo + half, le), device_id_type=MESH)

    def x_copy(source, offset):
        return pltpu.make_async_remote_copy(
            src_ref=source, dst_ref=over_x, send_sem=x_s, recv_sem=x_r,
            device_id=(la, lo + offset, le), device_id_type=MESH)

    def back_copy():
        return pltpu.make_async_remote_copy(
            src_ref=through, dst_ref=before.at[rest], send_sem=back_s, recv_sem=back_r,
            device_id=(la, lo + 1, le), device_id_type=MESH)

    def far_copy(far, to_odd):
        return pltpu.make_async_remote_copy(
            src_ref=joint, dst_ref=earlier.at[far - 1],
            send_sem=far_s.at[far - 1, to_odd], recv_sem=far_r.at[far - 1],
            device_id=(la, lo + 2 * far - 1 + to_odd, le), device_id_type=MESH)

    low_even = even & (lo < half)

    def rest_0():
        @pl.when(odd)
        def _():
            mate_copy(A).start()

    def rest_1():
        @pl.when(even)
        def _():
            mate_copy(A).wait_recv()

            @pl.loop(0, EDGE)
            def _(q):
                pair[q] = tot[q] + mate[q]

        @pl.when(lo == 0)
        def _():
            x_copy(pair, 2).start()

        @pl.when(low_even)
        def _():
            z_copy().start()

    def rest_2():
        @pl.when(lo == half)
        def _():
            z_copy().wait_recv()

            @pl.loop(0, EDGE)
            def _(q):
                pair[q] = pair[q] + over_z[q]

            x_copy(pair, 2).start()

        @pl.when(lo == half + 2)
        def _():
            z_copy().wait_recv()
            x_copy(over_z, -2).start()

    def rest_3():
        @pl.when(even & (lo > 0))
        def _():
            x_copy(pair, 2).wait_recv()

        @pl.when(lo == 0)
        def _():
            @pl.loop(0, EDGE)
            def _(q):
                before[q] = zero_row

        @pl.when(even & (lo > 0))
        def _():
            @pl.loop(0, EDGE)
            def _(q):
                before[q] = over_x[q]

        @pl.when(even & (lo >= half))
        def _():
            @pl.loop(0, EDGE)
            def _(q):
                before[q] = before[q] + over_z[q]

        @pl.when(even)
        def _():
            @pl.loop(0, EDGE)
            def _(q):
                through[q] = before[q] + tot[q]

            back_copy().start()

    def edge_0():
        @pl.when(even)
        def _():
            mate_copy(B).start()

    FARS = (3, 1, 2)

    def edge_1():
        @pl.when(odd)
        def _():
            mate_copy(B).wait_recv()
            joint[...] = tot[EDGE] + mate[EDGE]
            for far in FARS:
                @pl.when(lo + 2 * far < lon_size)
                def _():
                    far_copy(far, 1).start()
                    far_copy(far, 0).start()

    def edge_2():
        before[EDGE] = zero_row
        for far in range(1, slots):
            @pl.when(lo >= 2 * far)
            def _():
                far_copy(far, 1).wait_recv()
                before[EDGE] = before[EDGE] + earlier[far - 1]

        @pl.when(odd)
        def _():
            before[EDGE] = before[EDGE] + mate[EDGE]

    def prefix_end():
        @pl.when(odd)
        def _():
            back_copy().wait_recv()
            mate_copy(A).wait_send()
            for far in FARS:
                @pl.when(lo + 2 * far < lon_size)
                def _():
                    far_copy(far, 1).wait_send()
                    far_copy(far, 0).wait_send()

        @pl.when(even)
        def _():
            back_copy().wait_send()
            mate_copy(B).wait_send()

        @pl.when(low_even)
        def _():
            z_copy().wait_send()

        @pl.when(among((0, half, half + 2)))
        def _():
            x_copy(pair, 2).wait_send()

    def send_lat(tick):
        if tick >= CHUNKS:
            lat_copy(tick - CHUNKS).wait_send()
        lat_copy(tick).start()

    load(EDGE).wait()
    send_lat(0)
    send_lat(1)
    for p in (0, 3, 1, 2):
        load_pair(1, p).start()
        load_pair(2, p).start()
    send_lev(0, LAST)
    for side in range(2):
        send_near(0, side)

    @pl.loop(0, N)
    def _(i):
        for b in range(2):
            s[b, 0, i + 1, cells, :] = zero_row

    for side, row in ((0, 0), (1, N + 1)):
        @pl.when(jnp.logical_not(has_lon[side]))
        def _():
            @pl.loop(0, Q)
            def _(q):
                for b in range(2):
                    s[b, q + 1, row, cells, :] = zero_row

    for side, cell in ((0, PAD - 1), (1, TOP)):
        @pl.when(jnp.logical_not(has_lev[side]))
        def _():
            @pl.loop(0, Q)
            def _(q):
                @pl.loop(0, N)
                def _(i):
                    for b in range(2):
                        s[b, q + 1, i + 1, pl.ds(cell, 1), :] = zero_cell

    for g in range(LAST):
        q0, planes = GROUPS[g]
        for q in range(q0, q0 + planes):
            load(q).wait()
        send_lev(0, g)
        send_lon(0, g)
        if g < 2:
            send_lat(g + 2)

    for t in range(STEPS):
        final = t == STEPS - 1
        for n in range(CHUNKS):
            tick = t * CHUNKS + n
            lat_copy(tick).wait_recv()
            if tick + WINDOW < TICKS:
                send_lat(tick + WINDOW)
            if n < 2:
                @pl.when(wide[n])
                def _():
                    turn_copy(t, n).start()
            if t == 0 and n in (1, 4):
                pass_on(0, {1: 1, 4: 3}[n])
            if not final and n in (4, 7):
                pass_on(t + 1, {4: 1, 7: 3}[n])
            for m in LATE.get(n, ()):
                if m == 2:
                    if t == 0:
                        load_pair(1, 3).wait()
                        load_pair(2, 3).wait()
                    arrived_lev(t, LAST)
                    if t > 0:
                        sent_lev(t - 1, LAST)
                        sent_lon(t - 1, LAST)
                if m < 2:
                    arrived_lon(t, LAST, 1 - m)

                    @pl.when(wide[m])
                    def _():
                        turn_copy(t, m).wait_send()
                update_chunk(t, m)
                if not final and m < 2:
                    send_near(t + 1, m)
            planes = ((n,) if n < EDGE else ()) if not final else tuple(q for q in (2 * n, 2 * n + 1) if q < EDGE)
            for q in planes:
                g = q // 2
                first, count = GROUPS[g]
                if q == first:
                    if t == 0 and g < 3:
                        load_pair(1, g).wait()
                        load_pair(2, g).wait()
                    arrived_lev(t, g)
                    for side in range(2):
                        arrived_lon(t, g, side)
                    if t > 0:
                        sent_lev(t - 1, g)
                        sent_lon(t - 1, g)
                update_plane(t, q)
                if not final and q == first + count - 1:
                    send_lev(t + 1, g)
                    send_lon(t + 1, g)
            if final and n in (3, 4, 6):
                (rest_0, rest_1, rest_2)[(3, 4, 6).index(n)]()
        if not final:
            send_lev(t + 1, LAST)
    edge_0()
    edge_1()
    rest_3()
    edge_2()
    for n in range(CHUNKS):
        lat_copy(TICKS - CHUNKS + n).wait_send()
    for g in range(len(GROUPS)):
        sent_lev(STEPS - 1, g)
        sent_lon(STEPS - 1, g)
    for t in (STEPS - 2, STEPS - 1):
        for g in RELAY:
            for side in range(2):
                @pl.when(keeper[side])
                def _():
                    pass_copy(t, g, side).wait_send()
    prefix_end()


def finish(last, before, totals, end, run, t_sem, c_sem):
    la = lax.axis_index("lat")
    scale = 1.0 / (N * lax.axis_size("lon"))

    def place(q):
        return q + la * (Q - 1 - 2 * q)

    def put_end(p):
        planes = pl.ds(p * (Q // PIECES), Q // PIECES)
        return pltpu.make_async_copy(last.at[planes], end.at[planes], t_sem.at[p])

    def put_totals(q):
        return pltpu.make_async_copy(run.at[q], totals.at[place(q)], c_sem.at[q])

    for p in range(PIECES):
        put_end(p).start()
    for q in range(Q):
        def row(i, total):
            total = total + last[place(q), i]
            run[q, i] = total * scale
            return total
        lax.fori_loop(0, N, row, before[q])
        put_totals(q).start()
    for p in range(PIECES):
        put_end(p).wait()
    for q in range(Q):
        put_totals(q).wait()


def per_device(x, d, f):
    hbm = pl.BlockSpec(memory_space=pltpu.HBM)
    vmem = pl.BlockSpec(memory_space=pltpu.VMEM)
    slots = lax.axis_size("lon") // 2
    dma = pltpu.SemaphoreType.DMA
    block = (Q, N, K, M)
    part = (Q, K, M)
    f32 = jnp.float32
    last, before = pl.pallas_call(
        exchange,
        out_shape=(pltpu.VMEM(block, f32), pltpu.VMEM(part, f32)),
        in_specs=[hbm] * 3,
        out_specs=(vmem, vmem),
        scratch_shapes=[
            pltpu.VMEM((2, Q + 2, N + 2, K + 2 * PAD, M), f32),
            pltpu.VMEM(block, f32),
            pltpu.VMEM(block, f32),
            pltpu.VMEM((STEPS, 2 * len(RELAY), K, M), f32),
            pltpu.VMEM(part, f32),
            pltpu.VMEM(part, f32),
            pltpu.VMEM((EDGE, K, M), f32),
            pltpu.VMEM((K, M), f32),
            pltpu.VMEM((EDGE, K, M), f32),
            pltpu.VMEM((EDGE, K, M), f32),
            pltpu.VMEM((EDGE, K, M), f32),
            pltpu.VMEM((slots - 1, K, M), f32),
            dma((Q,)), dma((2, Q // 2)),
            dma((CHUNKS,)), dma((CHUNKS,)),
            dma((2, len(GROUPS), 2)), dma((2, len(GROUPS), 2)),
            dma((2, len(GROUPS), 2)), dma((2, len(GROUPS), 2)),
            dma((2, len(RELAY))), dma((2, len(RELAY))), dma,
            dma((2,)), dma((2,)), dma, dma, dma, dma, dma, dma,
            dma((slots - 1, 2)), dma((slots - 1,)),
        ],
        compiler_params=pltpu.CompilerParams(
            collective_id=0, has_side_effects=True, vmem_limit_bytes=52 * 1024 * 1024),
        name="exchange",
    )(x, d, f)
    totals, end = pl.pallas_call(
        finish,
        out_shape=(jax.ShapeDtypeStruct(block, f32), jax.ShapeDtypeStruct(block, f32)),
        in_specs=[vmem, vmem],
        out_specs=(hbm, hbm),
        scratch_shapes=[pltpu.VMEM(block, f32), dma((PIECES,)), dma((Q,))],
        compiler_params=pltpu.CompilerParams(vmem_limit_bytes=16 * 1024 * 1024),
        name="finish",
    )(last, before)
    return totals, end


def solution(mesh):
    spec = P("lat", "lon", "lev", None)
    return jax.shard_map(
        per_device, mesh=mesh, in_specs=(spec,) * 3, out_specs=(spec, spec), check_vma=False)
```

time: 129 us -> 127 us (0.984)
    pallas_call x1, Pallas kernels: 122 us -> 120 us  [per_device(): pl.pallas_call(exchange, out_shape=(pltpu.VMEM(block, f32), pltpu.VMEM(pa...]
where the time goes in v3:
time: 127 us
  Pallas kernels  126 us (99%)
    pallas_call x1, Pallas kernels, per_device(): pl.pallas_call(exchange, out_shape=(pltpu.VMEM(block, f32), pltpu.VMEM(pa...  120 us
    pallas_call x1, Pallas kernels, per_device(): pl.pallas_call(finish, out_shape=(jax.ShapeDtypeStruct(block, f32), jax.S...  5.93 us

profile of v3, /device:TPU:56, one launch (start us, length us, event | category | flops | bytes accessed | tf_op | source)
XLA Modules:
  0.0 126.7 jit_solution(6497169832957468385)
XLA Ops:
  0.6 120.2 %exchange.1 = (f32[8,32,64,128]{3,2,1,0:T(8,128)S(1)}, f32[8,64,128]{2,1,0:T(8,128)S(1)}) custom-call(f32[8,32,64,128]{3,2,1,0:T(8,128)} %x.1, f32[8,32,64,128]{3,2,1,0:T(8,128)} %d.1, f32[8,32,64,128]{3,2,1,0:T(8,128)} %f.1), custom_call_target="tpu_custom_call" | custom-call | tf_op jit(solution)/shard_map/exchange/pallas_call | solution.py:560
  120.8 5.9 %finish.1 = (f32[8,32,64,128]{3,2,1,0:T(8,128)}, f32[8,32,64,128]{3,2,1,0:T(8,128)}) custom-call(f32[8,32,64,128]{3,2,1,0:T(8,128)S(1)} %get-tuple-element.4.last, f32[8,64,128]{2,1,0:T(8,128)S(1)} %get-tuple-element.5.before), custom_call_target="tpu_custom_call" | custom-call | tf_op jit(solution)/shard_map/finish/pallas_call | solution.py:590

commit v4 on v3

--- a/solution.py
+++ b/solution.py
@@ -16,12 +16,13 @@
 ORDER = (0, 7, 1, 2, 3, 4, 5, 6)
 WINDOW = 4
 TICKS = STEPS * CHUNKS
-GROUPS = ((0, 2), (2, 2), (4, 2), (6, 1), (7, 1))
+GROUPS = ((0, 4), (4, 3), (7, 1))
 LAST = len(GROUPS) - 1
-RELAY = (1, 3)
+RELAY = (1,)
 LATE = {2: (2, 0), 3: (3, 1), 4: (4,), 5: (5,), 6: (6,), 7: (7,)}
 PIECES = 4
 A, B = 0, 1
+PASS = 5
 PLANES = ((0, Q - 1), (Q - 1, 1))
 GREET = ((1, range(7)), (2, (0, 1, 3, 4, 5)), (3, (0, 1, 3, 4)), (4, (0, 1, 2, 3)), (5, (1,)), (6, (1,)))
 
@@ -112,7 +113,7 @@
 
     def held(t, g):
         r = RELAY.index(g)
-        return hold.at[t, pl.ds(2 * r, GROUPS[g][1])], t % 2, r
+        return hold.at[t, r, pl.ds(0, GROUPS[g][1])], t % 2, r
 
     def hold_copy(t, g, side):
         buffer, b, r = held(t, g)
@@ -444,13 +445,34 @@
             load(q).wait()
         send_lev(0, g)
         send_lon(0, g)
-        if g < 2:
-            send_lat(g + 2)
+        send_lat(g + 2)
+
+    def update_planes(t, planes):
+        for q in planes:
+            g = q // 4
+            q0, n = GROUPS[g]
+            if t == 0 and q % 2 == 0 and q // 2 < 3:
+                for array in (1, 2):
+                    load_pair(array, q // 2).wait()
+            if q == q0:
+                arrived_lev(t, g)
+                for side in range(2):
+                    arrived_lon(t, g, side)
+                if t > 0:
+                    sent_lev(t - 1, g)
+                    sent_lon(t - 1, g)
+            update_plane(t, q)
+            if t < STEPS - 1 and q == q0 + n - 1:
+                send_lev(t + 1, g)
+                send_lon(t + 1, g)
 
     for t in range(STEPS):
         final = t == STEPS - 1
         for n in range(CHUNKS):
             tick = t * CHUNKS + n
+            if final and n == 0:
+                update_planes(t, range(EDGE))
+                rest_0()
             lat_copy(tick).wait_recv()
             if tick + WINDOW < TICKS:
                 send_lat(tick + WINDOW)
@@ -458,15 +480,15 @@
                 @pl.when(wide[n])
                 def _():
                     turn_copy(t, n).start()
-            if t == 0 and n in (1, 4):
-                pass_on(0, {1: 1, 4: 3}[n])
-            if not final and n in (4, 7):
-                pass_on(t + 1, {4: 1, 7: 3}[n])
+            if t == 0 and n == 1:
+                pass_on(0, RELAY[0])
+            if not final and n == PASS:
+                pass_on(t + 1, RELAY[0])
             for m in LATE.get(n, ()):
                 if m == 2:
                     if t == 0:
-                        load_pair(1, 3).wait()
-                        load_pair(2, 3).wait()
+                        for array in (1, 2):
+                            load_pair(array, 3).wait()
                     arrived_lev(t, LAST)
                     if t > 0:
                         sent_lev(t - 1, LAST)
@@ -480,26 +502,12 @@
                 update_chunk(t, m)
                 if not final and m < 2:
                     send_near(t + 1, m)
-            planes = ((n,) if n < EDGE else ()) if not final else tuple(q for q in (2 * n, 2 * n + 1) if q < EDGE)
-            for q in planes:
-                g = q // 2
-                first, count = GROUPS[g]
-                if q == first:
-                    if t == 0 and g < 3:
-                        load_pair(1, g).wait()
-                        load_pair(2, g).wait()
-                    arrived_lev(t, g)
-                    for side in range(2):
-                        arrived_lon(t, g, side)
-                    if t > 0:
-                        sent_lev(t - 1, g)
-                        sent_lon(t - 1, g)
-                update_plane(t, q)
-                if not final and q == first + count - 1:
-                    send_lev(t + 1, g)
-                    send_lon(t + 1, g)
-            if final and n in (3, 4, 6):
-                (rest_0, rest_1, rest_2)[(3, 4, 6).index(n)]()
+            if not final:
+                update_planes(t, [q for q in (2 * n, 2 * n + 1) if q < EDGE])
+            if final and n == 2:
+                rest_1()
+            if final and n == 4:
+                rest_2()
         if not final:
             send_lev(t + 1, LAST)
     edge_0()
@@ -566,7 +574,7 @@
             pltpu.VMEM((2, Q + 2, N + 2, K + 2 * PAD, M), f32),
             pltpu.VMEM(block, f32),
             pltpu.VMEM(block, f32),
-            pltpu.VMEM((STEPS, 2 * len(RELAY), K, M), f32),
+            pltpu.VMEM((STEPS, len(RELAY), 3, K, M), f32),
             pltpu.VMEM(part, f32),
             pltpu.VMEM(part, f32),
             pltpu.VMEM((EDGE, K, M), f32),

time: 127 us -> 124 us (0.976)
  Pallas kernels: 126 us -> 123 us
    pallas_call x1, Pallas kernels: 120 us -> 117 us  [per_device(): pl.pallas_call(exchange, out_shape=(pltpu.VMEM(block, f32), pltpu.VMEM(pa...]
where the time goes in v4:
time: 124 us
  Pallas kernels  123 us (99%)
    pallas_call x1, Pallas kernels, per_device(): pl.pallas_call(exchange, out_shape=(pltpu.VMEM(block, f32), pltpu.VMEM(pa...  117 us
    pallas_call x1, Pallas kernels, per_device(): pl.pallas_call(finish, out_shape=(jax.ShapeDtypeStruct(block, f32), jax.S...  5.93 us

profile of v4, /device:TPU:56, one launch (start us, length us, event | category | flops | bytes accessed | tf_op | source)
XLA Modules:
  0.0 123.6 jit_solution(5052405293463666465)
XLA Ops:
  0.6 117.0 %exchange.1 = (f32[8,32,64,128]{3,2,1,0:T(8,128)S(1)}, f32[8,64,128]{2,1,0:T(8,128)S(1)}) custom-call(f32[8,32,64,128]{3,2,1,0:T(8,128)} %x.1, f32[8,32,64,128]{3,2,1,0:T(8,128)} %d.1, f32[8,32,64,128]{3,2,1,0:T(8,128)} %f.1), custom_call_target="tpu_custom_call" | custom-call | tf_op jit(solution)/shard_map/exchange/pallas_call | solution.py:568
  117.7 5.9 %finish.1 = (f32[8,32,64,128]{3,2,1,0:T(8,128)}, f32[8,32,64,128]{3,2,1,0:T(8,128)}) custom-call(f32[8,32,64,128]{3,2,1,0:T(8,128)S(1)} %get-tuple-element.4.last, f32[8,64,128]{2,1,0:T(8,128)S(1)} %get-tuple-element.5.before), custom_call_target="tpu_custom_call" | custom-call | tf_op jit(solution)/shard_map/finish/pallas_call | solution.py:598

commit v5 on v4

--- a/solution.py
+++ b/solution.py
@@ -1,3 +1,5 @@
+import functools
+
 import jax
 import jax.numpy as jnp
 from jax import lax
@@ -27,9 +29,19 @@
 GREET = ((1, range(7)), (2, (0, 1, 3, 4, 5)), (3, (0, 1, 3, 4)), (4, (0, 1, 2, 3)), (5, (1,)), (6, (1,)))
 
 
-def exchange(x, d, f, last, before, s, dv, fv, hold, tot, mate, pair, joint, over_z, over_x, through, earlier,
-             in_sem, pair_sem, lat_s, lat_r, lon_s, lon_r, lev_s, lev_r, hold_s, hold_r, turn_s,
-             mate_s, mate_r, z_s, z_r, x_s, x_r, back_s, back_r, far_s, far_r):
+def exchange(*refs):
+    dma = pltpu.SemaphoreType.DMA
+    groups, slots = len(GROUPS), lax.axis_size("lon") // 2
+    own = (dma((Q,)), dma((2, Q // 2)), dma((CHUNKS,)), dma((2, groups, 2)), dma((2, groups, 2)),
+           dma((2, len(RELAY))), dma, dma((2,)), dma, dma, dma, dma((slots - 1, 2)),
+           dma((CHUNKS,)), dma((2, groups, 2)), dma((2, groups, 2)), dma((2, len(RELAY))),
+           dma((2,)), dma, dma, dma, dma((slots - 1,)))
+    pl.run_scoped(functools.partial(exchange_with, refs), *own)
+
+
+def exchange_with(refs, in_sem, pair_sem, lat_s, lon_s, lev_s, hold_s, turn_s, mate_s, z_s, x_s, back_s, far_s,
+                  lat_r, lon_r, lev_r, hold_r, mate_r, z_r, x_r, back_r, far_r):
+    (x, d, f, last, before, s, dv, fv, hold, tot, mate, pair, joint, over_z, over_x, through, earlier) = refs
     la, lo, le = lax.axis_index("lat"), lax.axis_index("lon"), lax.axis_index("lev")
     lon_size, lev_size = lax.axis_size("lon"), lax.axis_size("lev")
     half = lon_size // 2
@@ -528,7 +540,12 @@
     prefix_end()
 
 
-def finish(last, before, totals, end, run, t_sem, c_sem):
+def finish(*refs):
+    dma = pltpu.SemaphoreType.DMA
+    pl.run_scoped(functools.partial(finish_with, *refs), dma((PIECES,)), dma((Q,)))
+
+
+def finish_with(last, before, totals, end, run, t_sem, c_sem):
     la = lax.axis_index("lat")
     scale = 1.0 / (N * lax.axis_size("lon"))
 
@@ -561,7 +578,6 @@
     hbm = pl.BlockSpec(memory_space=pltpu.HBM)
     vmem = pl.BlockSpec(memory_space=pltpu.VMEM)
     slots = lax.axis_size("lon") // 2
-    dma = pltpu.SemaphoreType.DMA
     block = (Q, N, K, M)
     part = (Q, K, M)
     f32 = jnp.float32
@@ -583,13 +599,6 @@
             pltpu.VMEM((EDGE, K, M), f32),
             pltpu.VMEM((EDGE, K, M), f32),
             pltpu.VMEM((slots - 1, K, M), f32),
-            dma((Q,)), dma((2, Q // 2)),
-            dma((CHUNKS,)), dma((CHUNKS,)),
-            dma((2, len(GROUPS), 2)), dma((2, len(GROUPS), 2)),
-            dma((2, len(GROUPS), 2)), dma((2, len(GROUPS), 2)),
-            dma((2, len(RELAY))), dma((2, len(RELAY))), dma,
-            dma((2,)), dma((2,)), dma, dma, dma, dma, dma, dma,
-            dma((slots - 1, 2)), dma((slots - 1,)),
         ],
         compiler_params=pltpu.CompilerParams(
             collective_id=0, has_side_effects=True, vmem_limit_bytes=52 * 1024 * 1024),
@@ -600,7 +609,7 @@
         out_shape=(jax.ShapeDtypeStruct(block, f32), jax.ShapeDtypeStruct(block, f32)),
         in_specs=[vmem, vmem],
         out_specs=(hbm, hbm),
-        scratch_shapes=[pltpu.VMEM(block, f32), dma((PIECES,)), dma((Q,))],
+        scratch_shapes=[pltpu.VMEM(block, f32)],
         compiler_params=pltpu.CompilerParams(vmem_limit_bytes=16 * 1024 * 1024),
         name="finish",
     )(last, before)

time: 124 us -> 123 us (level)
  no operation moved by 1% of the time
where the time goes in v5:
time: 123 us
  Pallas kernels  122 us (99%)
    pallas_call x1, Pallas kernels, per_device(): pl.pallas_call(exchange, out_shape=(pltpu.VMEM(block, f32), pltpu.VMEM(pa...  116 us
    pallas_call x1, Pallas kernels, per_device(): pl.pallas_call(finish, out_shape=(jax.ShapeDtypeStruct(block, f32), jax.S...  5.82 us

profile of v5, /device:TPU:56, one launch (start us, length us, event | category | flops | bytes accessed | tf_op | source)
XLA Modules:
  0.0 122.6 jit_solution(4006437716045876396)
XLA Ops:
  0.6 116.1 %exchange.1 = (f32[8,32,64,128]{3,2,1,0:T(8,128)S(1)}, f32[8,64,128]{2,1,0:T(8,128)S(1)}) custom-call(f32[8,32,64,128]{3,2,1,0:T(8,128)} %refs_0_.1, f32[8,32,64,128]{3,2,1,0:T(8,128)} %refs_1_.1, f32[8,32,64,128]{3,2,1,0:T(8,128)} %refs_2_.1), custom_call_target="tpu_custom_call" | custom-call | tf_op jit(solution)/shard_map/exchange/pallas_call | solution.py:584
  116.7 5.8 %finish.1 = (f32[8,32,64,128]{3,2,1,0:T(8,128)}, f32[8,32,64,128]{3,2,1,0:T(8,128)}) custom-call(f32[8,32,64,128]{3,2,1,0:T(8,128)S(1)} %get-tuple-element.4.refs_0_, f32[8,64,128]{2,1,0:T(8,128)S(1)} %get-tuple-element.5.refs_1_), custom_call_target="tpu_custom_call" | custom-call | tf_op jit(solution)/shard_map/finish/pallas_call | solution.py:607

commit v6 on v5

--- a/solution.py
+++ b/solution.py
@@ -16,7 +16,7 @@
 CHUNKS = 8
 ROWS = N // CHUNKS
 ORDER = (0, 7, 1, 2, 3, 4, 5, 6)
-WINDOW = 4
+WINDOW = 5
 TICKS = STEPS * CHUNKS
 GROUPS = ((0, 4), (4, 3), (7, 1))
 LAST = len(GROUPS) - 1
@@ -32,9 +32,9 @@
 def exchange(*refs):
     dma = pltpu.SemaphoreType.DMA
     groups, slots = len(GROUPS), lax.axis_size("lon") // 2
-    own = (dma((Q,)), dma((2, Q // 2)), dma((CHUNKS,)), dma((2, groups, 2)), dma((2, groups, 2)),
+    own = (dma((Q,)), dma((2, Q // 2)), dma((TICKS,)), dma((2, groups, 2)), dma((2, groups, 2)),
            dma((2, len(RELAY))), dma, dma((2,)), dma, dma, dma, dma((slots - 1, 2)),
-           dma((CHUNKS,)), dma((2, groups, 2)), dma((2, groups, 2)), dma((2, len(RELAY))),
+           dma((TICKS,)), dma((2, groups, 2)), dma((2, groups, 2)), dma((2, len(RELAY))),
            dma((2,)), dma, dma, dma, dma((slots - 1,)))
     pl.run_scoped(functools.partial(exchange_with, refs), *own)
 
@@ -108,7 +108,7 @@
         return pltpu.make_async_remote_copy(
             src_ref=s.at[t % 2, Q, rows, cells, :],
             dst_ref=s.at[t % 2, Q + 1, rows, cells, :],
-            send_sem=lat_s.at[tick % CHUNKS], recv_sem=lat_r.at[tick % CHUNKS],
+            send_sem=lat_s.at[tick], recv_sem=lat_r.at[tick],
             device_id=(1 - la, lo, le), device_id_type=MESH)
 
     FROM, TO = (1, N), (N + 1, 0)
@@ -458,6 +458,8 @@
         send_lev(0, g)
         send_lon(0, g)
         send_lat(g + 2)
+    for tick in range(4, WINDOW):
+        send_lat(tick)
 
     def update_planes(t, planes):
         for q in planes:

time: 123 us -> 123 us (level)
  no operation moved by 1% of the time
where the time goes in v6:
time: 123 us
  Pallas kernels  122 us (99%)
    pallas_call x1, Pallas kernels, per_device(): pl.pallas_call(exchange, out_shape=(pltpu.VMEM(block, f32), pltpu.VMEM(pa...  116 us
    pallas_call x1, Pallas kernels, per_device(): pl.pallas_call(finish, out_shape=(jax.ShapeDtypeStruct(block, f32), jax.S...  5.82 us

profile of v6, /device:TPU:56, one launch (start us, length us, event | category | flops | bytes accessed | tf_op | source)
XLA Modules:
  0.0 122.6 jit_solution(16286574663931785530)
XLA Ops:
  0.6 116.1 %exchange.1 = (f32[8,32,64,128]{3,2,1,0:T(8,128)S(1)}, f32[8,64,128]{2,1,0:T(8,128)S(1)}) custom-call(f32[8,32,64,128]{3,2,1,0:T(8,128)} %refs_0_.1, f32[8,32,64,128]{3,2,1,0:T(8,128)} %refs_1_.1, f32[8,32,64,128]{3,2,1,0:T(8,128)} %refs_2_.1), custom_call_target="tpu_custom_call" | custom-call | tf_op jit(solution)/shard_map/exchange/pallas_call | solution.py:586
  116.7 5.8 %finish.1 = (f32[8,32,64,128]{3,2,1,0:T(8,128)}, f32[8,32,64,128]{3,2,1,0:T(8,128)}) custom-call(f32[8,32,64,128]{3,2,1,0:T(8,128)S(1)} %get-tuple-element.4.refs_0_, f32[8,64,128]{2,1,0:T(8,128)S(1)} %get-tuple-element.5.refs_1_), custom_call_target="tpu_custom_call" | custom-call | tf_op jit(solution)/shard_map/finish/pallas_call | solution.py:609

commit v7 on v6

--- a/solution.py
+++ b/solution.py
@@ -20,21 +20,21 @@
 TICKS = STEPS * CHUNKS
 GROUPS = ((0, 4), (4, 3), (7, 1))
 LAST = len(GROUPS) - 1
-RELAY = (1,)
+RELAY = ((1, 1), (0, 1), (0, 1), (1, 1))
 LATE = {2: (2, 0), 3: (3, 1), 4: (4,), 5: (5,), 6: (6,), 7: (7,)}
 PIECES = 4
 A, B = 0, 1
 PASS = 5
 PLANES = ((0, Q - 1), (Q - 1, 1))
-GREET = ((1, range(7)), (2, (0, 1, 3, 4, 5)), (3, (0, 1, 3, 4)), (4, (0, 1, 2, 3)), (5, (1,)), (6, (1,)))
+GREET = ((6, (1,)), (5, (1,)), (3, (0, 1, 3, 4)), (1, range(7)), (2, (0, 1, 3, 4, 5)), (4, (0, 1, 2, 3)))
 
 
 def exchange(*refs):
     dma = pltpu.SemaphoreType.DMA
     groups, slots = len(GROUPS), lax.axis_size("lon") // 2
     own = (dma((Q,)), dma((2, Q // 2)), dma((TICKS,)), dma((2, groups, 2)), dma((2, groups, 2)),
-           dma((2, len(RELAY))), dma, dma((2,)), dma, dma, dma, dma((slots - 1, 2)),
-           dma((TICKS,)), dma((2, groups, 2)), dma((2, groups, 2)), dma((2, len(RELAY))),
+           dma((2,)), dma, dma((2,)), dma, dma, dma, dma((slots - 1, 2)),
+           dma((TICKS,)), dma((2, groups, 2)), dma((2, groups, 2)), dma((STEPS,)),
            dma((2,)), dma, dma, dma, dma((slots - 1,)))
     pl.run_scoped(functools.partial(exchange_with, refs), *own)
 
@@ -77,17 +77,18 @@
             found = found | (lo == m)
         return found
 
-    greet((1 - la, lo, le))
     count = jnp.int32(1)
     peers = [
         (has_lev[0], (la, lo, le - 1)),
         (has_lev[1], (la, lo, le + 1)),
-        (wide[0], (1 - la, lo - 1, le)),
-        (wide[1], (1 - la, lo + 1, le)),
     ]
     for offset, lower in GREET:
         peers.append((among(lower), (la, lo + offset, le)))
         peers.append((among([m + offset for m in lower]), (la, lo - offset, le)))
+    peers += [
+        (wide[0], (1 - la, lo - 1, le)),
+        (wide[1], (1 - la, lo + 1, le)),
+    ]
     for there, dev in peers:
         count = count + there.astype(jnp.int32)
 
@@ -95,6 +96,7 @@
         def _():
             greet(dev)
 
+    greet((1 - la, lo, le))
     for q in range(EDGE):
         load(q).start()
     pl.semaphore_wait(barrier, count)
@@ -123,22 +125,18 @@
             send_sem=lon_s.at[t % 2, g, side], recv_sem=lon_r.at[t % 2, g, side],
             device_id=(la, lo + (-1, 1)[side], le), device_id_type=MESH)
 
-    def held(t, g):
-        r = RELAY.index(g)
-        return hold.at[t, r, pl.ds(0, GROUPS[g][1])], t % 2, r
-
-    def hold_copy(t, g, side):
-        buffer, b, r = held(t, g)
-        return pltpu.make_async_remote_copy(
-            src_ref=face(t, g, FROM[side]), dst_ref=buffer,
-            send_sem=lon_s.at[b, g, side], recv_sem=hold_r.at[b, r],
+    def hold_copy(t, side):
+        g = RELAY[t][side]
+        return pltpu.make_async_remote_copy(
+            src_ref=face(t, g, FROM[side]), dst_ref=hold.at[t, pl.ds(0, GROUPS[g][1])],
+            send_sem=lon_s.at[t % 2, g, side], recv_sem=hold_r.at[t],
             device_id=(la, lo + (-half, half)[side], le), device_id_type=MESH)
 
-    def pass_copy(t, g, side):
-        buffer, b, r = held(t, g)
-        return pltpu.make_async_remote_copy(
-            src_ref=buffer, dst_ref=face(t, g, TO[side]),
-            send_sem=hold_s.at[b, r], recv_sem=lon_r.at[b, g, side],
+    def pass_copy(t, side):
+        g = RELAY[t][side]
+        return pltpu.make_async_remote_copy(
+            src_ref=hold.at[t, pl.ds(0, GROUPS[g][1])], dst_ref=face(t, g, TO[side]),
+            send_sem=hold_s.at[t % 2], recv_sem=lon_r.at[t % 2, g, side],
             device_id=(la, lo + (half - 1, 1 - half)[side], le), device_id_type=MESH)
 
     def turn_copy(t, side):
@@ -168,14 +166,14 @@
 
     def send_lon(t, q):
         for side in range(2):
-            if q in RELAY:
+            if q == RELAY[t][side]:
                 @pl.when(has_lon[side] & jnp.logical_not(sender[side]))
                 def _():
                     lon_copy(t, q, side).start()
 
                 @pl.when(sender[side])
                 def _():
-                    hold_copy(t, q, side).start()
+                    hold_copy(t, side).start()
             else:
                 @pl.when(has_lon[side])
                 def _():
@@ -186,14 +184,14 @@
         def _():
             lon_copy(t, LAST, side).start()
 
-    def pass_on(t, q):
+    def pass_on(t):
         for side in range(2):
             @pl.when(keeper[side])
             def _():
                 if t > 1:
-                    pass_copy(t - 2, q, side).wait_send()
-                hold_copy(t, q, side).wait_recv()
-                pass_copy(t, q, side).start()
+                    pass_copy(t - 2, side).wait_send()
+                hold_copy(t, side).wait_recv()
+                pass_copy(t, side).start()
 
     def sent_lev(t, q):
         for side in range(2):
@@ -374,8 +372,8 @@
             for far in FARS:
                 @pl.when(lo + 2 * far < lon_size)
                 def _():
-                    far_copy(far, 1).start()
-                    far_copy(far, 0).start()
+                    for to_odd in ((0, 1) if far == 1 else (1, 0)):
+                        far_copy(far, to_odd).start()
 
     def edge_2():
         before[EDGE] = zero_row
@@ -495,9 +493,9 @@
                 def _():
                     turn_copy(t, n).start()
             if t == 0 and n == 1:
-                pass_on(0, RELAY[0])
+                pass_on(0)
             if not final and n == PASS:
-                pass_on(t + 1, RELAY[0])
+                pass_on(t + 1)
             for m in LATE.get(n, ()):
                 if m == 2:
                     if t == 0:
@@ -534,11 +532,10 @@
         sent_lev(STEPS - 1, g)
         sent_lon(STEPS - 1, g)
     for t in (STEPS - 2, STEPS - 1):
-        for g in RELAY:
-            for side in range(2):
-                @pl.when(keeper[side])
-                def _():
-                    pass_copy(t, g, side).wait_send()
+        for side in range(2):
+            @pl.when(keeper[side])
+            def _():
+                pass_copy(t, side).wait_send()
     prefix_end()
 
 
@@ -592,7 +589,7 @@
             pltpu.VMEM((2, Q + 2, N + 2, K + 2 * PAD, M), f32),
             pltpu.VMEM(block, f32),
             pltpu.VMEM(block, f32),
-            pltpu.VMEM((STEPS, len(RELAY), 3, K, M), f32),
+            pltpu.VMEM((STEPS, 4, K, M), f32),
             pltpu.VMEM(part, f32),
             pltpu.VMEM(part, f32),
             pltpu.VMEM((EDGE, K, M), f32),

time: 123 us -> 123 us (level)
  no operation moved by 1% of the time
where the time goes in v7:
time: 123 us; the launch traced here: 122 us
  Pallas kernels  122 us (99%)
    pallas_call x1, Pallas kernels, per_device(): pl.pallas_call(exchange, out_shape=(pltpu.VMEM(block, f32), pltpu.VMEM(pa...  116 us
    pallas_call x1, Pallas kernels, per_device(): pl.pallas_call(finish, out_shape=(jax.ShapeDtypeStruct(block, f32), jax.S...  5.82 us

profile of v7, /device:TPU:56, one launch (start us, length us, event | category | flops | bytes accessed | tf_op | source)
XLA Modules:
  0.0 122.2 jit_solution(5321852978992647581)
XLA Ops:
  0.6 115.7 %exchange.1 = (f32[8,32,64,128]{3,2,1,0:T(8,128)S(1)}, f32[8,64,128]{2,1,0:T(8,128)S(1)}) custom-call(f32[8,32,64,128]{3,2,1,0:T(8,128)} %refs_0_.1, f32[8,32,64,128]{3,2,1,0:T(8,128)} %refs_1_.1, f32[8,32,64,128]{3,2,1,0:T(8,128)} %refs_2_.1), custom_call_target="tpu_custom_call" | custom-call | tf_op jit(solution)/shard_map/exchange/pallas_call | solution.py:583
  116.4 5.8 %finish.1 = (f32[8,32,64,128]{3,2,1,0:T(8,128)}, f32[8,32,64,128]{3,2,1,0:T(8,128)}) custom-call(f32[8,32,64,128]{3,2,1,0:T(8,128)S(1)} %get-tuple-element.4.refs_0_, f32[8,64,128]{2,1,0:T(8,128)S(1)} %get-tuple-element.5.refs_1_), custom_call_target="tpu_custom_call" | custom-call | tf_op jit(solution)/shard_map/finish/pallas_call | solution.py:606
